TPU v7x, 512 devices: a whole 4x4x16 slice. The times are simulated.
512 devices in a mesh: pts: 32 (over x, y, core), cand: 16 (over z).
Axes of the slice: x: 4, y: 4, z: 16, core: 2. Of those that a mesh axis runs over, the one named last changes fastest.
Arguments:
- points: bfloat16 [32768, 1024], P('pts'), may hold values from -6 to 6
- weights: float32 [32768], P('pts'), may hold values from 0.5 to 5
- coverage: float32 [32768], P('pts'), may hold values from -0.5 to 1
- candidates: bfloat16 [16384, 1024], P('cand'), may hold values from -6 to 6
- picks: int32 [64], replicated, may hold values from 0 to 16383
Outputs:
- gains: float32 [16384], P('cand')
- top_gains: float32 [64], replicated
- new_coverage: float32 [32768], P('pts')
All inputs are finite; a program needn't handle non-finite values.
Results may differ from a plain program's by a relative error of at most 0.0003.
Values may be sent and summed in bfloat16 or wider, within the bound.
A program may use at most 64 MiB of HBM per device.

v0:
```python
import jax
import jax.numpy as jnp
from jax import lax
from jax.sharding import PartitionSpec as P

TOPK = 64


def from_everyone(x, axis):
    copies = jnp.broadcast_to(x, (lax.axis_size(axis), *x.shape))
    return lax.all_to_all(copies, axis, split_axis=0, concat_axis=0, tiled=True)


def over_copies(x, axis):
    return from_everyone(x, axis).sum(axis=0)


def combined_pairwise(pieces, combine):
    while len(jax.tree.leaves(pieces)[0]) > 1:
        pieces = jax.vmap(combine)(*(pieces[side::2] for side in (0, 1)))
    return pieces[0]


def joined_all(x, axis, combine):
    pieces = from_everyone(x, axis)
    return combined_pairwise(pieces, combine)


def taken_together(x, axis):
    return from_everyone(x, axis).max(axis=0)


def best_values(first, second):
    return lax.top_k(jnp.concatenate([first, second]), TOPK)[0]


def on_device(points, weights, coverage, candidates, picks):
    scale = points.shape[1] ** (-0.5)
    total = points.shape[0] * lax.axis_size("pts")
    cand_rows = candidates.shape[0]
    offset = lax.axis_index("cand") * cand_rows
    sims = jnp.dot(points, candidates.T, preferred_element_type=jnp.float32) * scale
    partial_value = (
        jnp.sum(weights[:, None] * jnp.maximum(sims - coverage[:, None], 0.0), axis=0) / total
    )
    gains = over_copies(partial_value, "pts")
    top_gains = joined_all(lax.top_k(gains, TOPK)[0], "cand", best_values)
    columns = offset + jnp.arange(cand_rows, dtype=jnp.int32)
    chosen = jnp.any(picks[:, None] == columns[None, :], axis=0)
    local_best = jnp.max(jnp.where(chosen[None, :], sims, -1e30), axis=1)
    best_sim = taken_together(local_best, "cand")
    new_coverage = jnp.maximum(coverage, best_sim)
    return (gains, top_gains, new_coverage)


def solution(mesh):
    placed = (P("pts", None), P("pts"), P("pts"), P("cand", None), P())
    return jax.shard_map(
        on_device, mesh=mesh, in_specs=placed, out_specs=(P("cand"), P(), P("pts")), check_vma=False
    )
```

profile of v0, /device:TPU:1, one launch (start us, length us, event | category | flops | bytes accessed | tf_op | source)
XLA Modules:
  0.0 69.8 jit_solution(17755846284915081702)
XLA Ops:
  0.6 0.0 copy-start
  0.7 0.9 %compare_reduce_fusion = pred[1024]{0:T(1024)(128)(4,1)S(1)} fusion(s32[1024]{0:T(1024)S(1)} %iota_add_fusion, s32[64]{0:T(128)} %param.9), kind=kLoop, calls=%fused_computation.2 | loop fusion | flops 130048 | bytes 5376 | tf_op jit(solution)/shard_map/reduce_or | solution.py:49
  1.6 0.7 copy-done
  2.2 4.4 %select_reduce_fusion = (f32[1024]{0:T(1024)S(1)}, f32[1024]{0:T(1024)S(1)}) fusion(pred[1024]{0:T(1024)(128)(4,1)S(1)} %compare_reduce_fusion, f32[1024]{0:T(1024)} %param.7, f32[1024]{0:T(1024)} %param.6, bf16[1024,1024]{1,0:T(8,128)(2,1)S(1)} %copy-done, bf16[1024,1024]{1,0:T(8,128)(2,1)} %param.8), kind=kOutput, calls=%fused_computation | convolution fusion | flops 2154821632 | bytes 4211712 | tf_op jit(solution)/shard_map/dot_general | solution.py:42
  6.6 0.1 broadcast_in_dim.26
  6.7 17.3 %all_to_all.21 = f32[32,1,1024]{2,1,0:T(1,128)S(1)} all-to-all(f32[32,1,1024]{2,1,0:T(1,128)S(1)} %broadcast_in_dim.26), channel_id=1, replica_groups=mesh['pts'=32,'cand'=16] {'pts'}, dimensions={0} | all-to-all | bytes 262144 | tf_op jit(solution)/shard_map/all_to_all | solution.py:11
  23.9 0.1 reduce_sum.19
  24.0 0.0 copy-start.1
  24.1 4.4 %top_k.36 = (f32[1024]{0:T(1024)S(1)}, s32[1024]{0:T(1024)}) sort(f32[1024]{0:T(1024)S(1)} %reduce_sum.19, s32[1024]{0:T(1024)S(1)} %iota.20), dimensions={0}, to_apply=%region_2.0 | sort | flops 10240 | bytes 16384 | tf_op jit(solution)/shard_map/top_k | solution.py:47
  28.5 24.8 %all_to_all.22 = f32[16,1,64]{2,1,0:T(1,128)S(1)} all-to-all(f32[16,1,64]{2,1,0:T(1,128)S(1)} %broadcast_in_dim.27), channel_id=1, replica_groups=mesh['pts'=32,'cand'=16] {'cand'}, dimensions={0} | all-to-all | bytes 8192 | tf_op jit(solution)/shard_map/all_to_all | solution.py:11
  53.3 0.7 broadcast_in_dim.30
  54.0 3.5 %all-to-all-start.2 = ((f32[16,1,1024]{2,1,0:T(1,128)}), f32[16,1,1024]{2,1,0:T(1,128)S(1)}, u32[]{:S(2)}, u32[]{:S(2)}) async-start(f32[16,1,1024]{2,1,0:T(1,128)} %broadcast_in_dim.30), calls=%async_computation.2 | async-start | bytes 131072 | tf_op jit(solution)/shard_map/all_to_all | solution.py:11
  57.5 0.1 pad_maximum_fusion
  57.6 2.6 %top_k.38 = (f32[8,128]{1,0:T(8,128)S(1)}, s32[8,128]{1,0:T(8,128)}) sort(f32[8,128]{1,0:T(8,128)S(1)} %pad_maximum_fusion, s32[8,128]{1,0:T(8,128)S(1)} %iota.21), dimensions={1}, to_apply=%region_3.4 | sort | flops 10240 | bytes 16384 | tf_op jit(solution)/shard_map/vmap()/top_k | solution.py:34
  60.3 0.1 pad_maximum_fusion.1
  60.4 2.6 %top_k.44 = (f32[4,128]{1,0:T(4,128)S(1)}, s32[4,128]{1,0:T(4,128)}) sort(f32[4,128]{1,0:T(4,128)S(1)} %pad_maximum_fusion.1, s32[4,128]{1,0:T(4,128)S(1)} %iota.22), dimensions={1}, to_apply=%region_4.5 | sort | flops 4608 | bytes 8192 | tf_op jit(solution)/shard_map/vmap()/top_k | solution.py:34
  63.0 0.1 pad_maximum_fusion.2
  63.1 2.6 %top_k.46 = (f32[2,128]{1,0:T(2,128)S(1)}, s32[2,128]{1,0:T(2,128)}) sort(f32[2,128]{1,0:T(2,128)S(1)} %pad_maximum_fusion.2, s32[2,128]{1,0:T(2,128)S(1)} %iota.23), dimensions={1}, to_apply=%region_5.6 | sort | flops 2048 | bytes 4096 | tf_op jit(solution)/shard_map/vmap()/top_k | solution.py:34
  65.7 0.1 pad_maximum_fusion.3
  65.8 2.6 %top_k.47 = (f32[1,128]{1,0:T(1,128)S(1)}, s32[1,128]{1,0:T(1,128)}) sort(f32[1,128]{1,0:T(1,128)S(1)} %pad_maximum_fusion.3, s32[1,128]{1,0:T(1,128)S(1)} %iota.24), dimensions={1}, to_apply=%region_6.7 | sort | flops 896 | bytes 2048 | tf_op jit(solution)/shard_map/vmap()/top_k | solution.py:34
  68.4 0.5 slice_bitcast_fusion
  68.9 0.2 all-to-all-done.2
  69.1 0.1 reduce_max.19
  69.2 0.6 max.11
  (19 shorter events, 0.2 us)
Async XLA Ops:
  0.6 1.6 %copy-start = (bf16[1024,1024]{1,0:T(8,128)(2,1)S(1)}, bf16[1024,1024]{1,0:T(8,128)(2,1)}, u32[]{:S(2)}) copy-start(bf16[1024,1024]{1,0:T(8,128)(2,1)} %param.5) | copy-start | bytes 6291460
  2.2 66.9 %copy-start.2 = (f32[1024]{0:T(1024)S(1)}, f32[1024]{0:T(1024)}, u32[]{:S(2)}) copy-start(f32[1024]{0:T(1024)} %param.7) | copy-start | bytes 12292
  24.0 45.7 %copy-start.1 = (f32[1024]{0:T(1024)}, f32[1024]{0:T(1024)S(1)}, u32[]{:S(2)}) copy-start(f32[1024]{0:T(1024)S(1)} %reduce_sum.19) | copy-start | bytes 12292
  54.0 15.1 %all-to-all-start.2 = ((f32[16,1,1024]{2,1,0:T(1,128)}), f32[16,1,1024]{2,1,0:T(1,128)S(1)}, u32[]{:S(2)}, u32[]{:S(2)}) async-start(f32[16,1,1024]{2,1,0:T(1,128)} %broadcast_in_dim.30), calls=%async_computation.2 | async-start | bytes 131072 | tf_op jit(solution)/shard_map/all_to_all | solution.py:11
where the time goes:
time: 70.6 us; the launch traced here: 69.8 us
  blocking collectives  42.1 us (60%)
  other arithmetic  16.8 us (24%)
  matrix products  4.35 us (6%)
  starting transfers between devices  3.5 us (5%)
  local copies, waits for them, and re-layouts  2.06 us (3%)
  between operations  0.71 us (1%)
    all_to_all x2, blocking collectives, from_everyone(): return lax.all_to_all(copies, axis, split_axis=0, concat_axis=0, tiled=True)  42.1 us
    top_k x4, other arithmetic, best_values(): return lax.top_k(jnp.concatenate([first, second]), TOPK)[0]  10.4 us
    top_k x1, other arithmetic, on_device(): top_gains = joined_all(lax.top_k(gains, TOPK)[0], 'cand', best_values)  4.43 us
    dot_general x1, matrix products, on_device(): jnp.dot(points, candidates.T, preferred_element_type=jnp.float32) * scale  4.35 us
    all_to_all x1, starting transfers between devices, from_everyone(): return lax.all_to_all(copies, axis, split_axis=0, concat_axis=0, tiled=True)  3.5 us
  transfers between devices with their start and end apart: 1, of which 1 were waited for; matrix products, arithmetic and copies ran while one was open for 16% of the time, Pallas kernels for 0%

commit v1 on v0

v1 whole, which is shorter than its diff:
```python
import functools

import jax
import jax.numpy as jnp
from jax import lax
from jax.experimental import pallas as pl
from jax.experimental.pallas import tpu as pltpu
from jax.sharding import PartitionSpec as P

TOPK = 64
LANES = 128
F32 = jnp.float32


def column_of(row):
    return jnp.broadcast_to(row, (LANES, LANES)).T


def best_sorted(rows_ref, col_ref):
    for k in range(8):
        col_ref[k * LANES:(k + 1) * LANES, :] = column_of(rows_ref[k:k + 1, :])
    rows = [jnp.broadcast_to(rows_ref[k:k + 1, :], (8, LANES)) for k in range(8)]

    def count(step, above):
        for part in range(8):
            start = pl.multiple_of(step * 64 + part * 8, 8)
            other = col_ref[pl.ds(start, 8), :]
            above = tuple(a + jnp.where(other > r, 1.0, 0.0) for a, r in zip(above, rows))
        return above

    above = lax.fori_loop(0, 16, count, tuple(jnp.zeros((8, LANES), F32) for _ in range(8)))
    above = [jnp.broadcast_to(jnp.sum(a, axis=0, keepdims=True), (8, LANES)) for a in above]
    sub = lax.broadcasted_iota(jnp.int32, (8, LANES), 0)
    lane = lax.rem(lax.broadcasted_iota(jnp.int32, (8, LANES), 1), TOPK)
    placed = jnp.zeros((8, LANES), F32)
    for block in range(8):
        place = (sub + block * 8).astype(F32)
        best = jnp.full((8, LANES), jnp.inf, F32)
        for a, r in zip(above, rows):
            best = jnp.minimum(best, jnp.where(a <= place, r, jnp.inf))
        best = jnp.min(best, axis=1, keepdims=True)
        placed = placed + jnp.where(lane == sub + block * 8, best, 0.0)
    return jnp.sum(placed, axis=0, keepdims=True)


def kernel(
    n_pts, n_cand,
    points_hbm, weights_hbm, cover_hbm, cand_hbm, picks_hbm,
    gains_ref, top_ref, ncov_ref,
    points, cands, weights, cover, picks, wcol, ccol, bias, maxes, acc, col,
    part_out, part_in, cov_out, cov_in, top_out, top_in, rows,
    in_sem, p_send, p_recv, c_send, c_recv, t_send, t_recv,
):
    n = points.shape[0]
    m = cands.shape[0]
    me_p = lax.axis_index("pts")
    me_c = lax.axis_index("cand")

    copies = [
        pltpu.make_async_copy(cover_hbm, cover, in_sem.at[0]),
        pltpu.make_async_copy(weights_hbm, weights, in_sem.at[1]),
        pltpu.make_async_copy(picks_hbm, picks, in_sem.at[2]),
        pltpu.make_async_copy(cand_hbm.at[pl.ds(0, 256)], cands.at[pl.ds(0, 256)], in_sem.at[3]),
        pltpu.make_async_copy(points_hbm, points, in_sem.at[4]),
        pltpu.make_async_copy(cand_hbm.at[pl.ds(256, 768)], cands.at[pl.ds(256, 768)], in_sem.at[5]),
    ]
    for copy in copies:
        copy.start()

    barrier = pltpu.get_barrier_semaphore()
    for k in range(1, n_pts):
        pl.semaphore_signal(barrier, 1, device_id={"pts": lax.rem(me_p + k, n_pts)}, device_id_type=pl.DeviceIdType.MESH)
    for k in range(1, n_cand):
        pl.semaphore_signal(barrier, 1, device_id={"cand": lax.rem(me_c + k, n_cand)}, device_id_type=pl.DeviceIdType.MESH)

    copies[0].wait()
    copies[1].wait()
    for k in range(8):
        ccol[k * LANES:(k + 1) * LANES, :] = column_of(cover[k:k + 1, :] * 32.0)
        wcol[k * LANES:(k + 1) * LANES, :] = column_of(weights[k:k + 1, :] * (2.0 ** -20))
    copies[2].wait()
    column = (
        me_c * m
        + lax.broadcasted_iota(jnp.int32, (8, LANES), 0) * LANES
        + lax.broadcasted_iota(jnp.int32, (8, LANES), 1)
    )
    mask = jnp.full((8, LANES), -1e30, F32)
    for k in range(TOPK):
        mask = jnp.where(column == picks[k], 0.0, mask)
    bias[...] = mask
    copies[3].wait()
    copies[4].wait()

    block = 256
    for tile in range(4):
        if tile == 1:
            copies[5].wait()
        rhs = cands[tile * 256:(tile + 1) * 256, :]
        halves = [bias[2 * tile + h:2 * tile + h + 1, :] for h in range(2)]
        sums = [jnp.zeros((8, LANES), F32) for _ in range(2)]
        for b in range(n // block):
            at = slice(b * block, (b + 1) * block)
            sims = lax.dot_general(
                points[at, :], rhs, (((1,), (1,)), ((), ())), preferred_element_type=F32
            )
            high = None
            for h in range(2):
                s = sims[:, h * LANES:(h + 1) * LANES]
                t = jnp.maximum(s - ccol[at, :], 0.0) * wcol[at, :]
                sums[h] = sums[h] + jnp.sum(t.reshape(block // 8, 8, LANES), axis=0)
                masked = s + halves[h]
                high = masked if high is None else jnp.maximum(high, masked)
            if tile == 0:
                maxes[at, :] = high
            else:
                maxes[at, :] = jnp.maximum(maxes[at, :], high)
        for h in range(2):
            part_out[2 * tile + h:2 * tile + h + 1, :] = jnp.sum(sums[h], axis=0, keepdims=True)

    pl.semaphore_wait(barrier, n_pts - 1 + n_cand - 1)
    part_in[me_p] = part_out[...]
    for k in range(1, n_pts):
        pltpu.make_async_remote_copy(
            part_out, part_in.at[me_p], p_send, p_recv,
            device_id={"pts": lax.rem(me_p + k, n_pts)}, device_id_type=pl.DeviceIdType.MESH,
        ).start()
    for k in range(8):
        high = maxes[k * LANES:(k + 1) * LANES, :].T
        cov_out[k:k + 1, :] = jnp.max(high, axis=0, keepdims=True) * (2.0 ** -5)
    cov_in[me_c] = cov_out[...]
    for k in range(1, n_cand):
        pltpu.make_async_remote_copy(
            cov_out, cov_in.at[me_c], c_send, c_recv,
            device_id={"cand": lax.rem(me_c + k, n_cand)}, device_id_type=pl.DeviceIdType.MESH,
        ).start()

    some = part_in.at[pl.ds(0, n_pts - 1)]
    pltpu.make_async_copy(some, some, p_recv).wait()
    total = part_in[0]
    for k in range(1, n_pts):
        total = total + part_in[k]
    rows[...] = total
    gains_ref[...] = total
    top_out[...] = best_sorted(rows, col)
    top_in[me_c] = top_out[...]
    for k in range(1, n_cand):
        pltpu.make_async_remote_copy(
            top_out, top_in.at[me_c], t_send, t_recv,
            device_id={"cand": lax.rem(me_c + k, n_cand)}, device_id_type=pl.DeviceIdType.MESH,
        ).start()

    some = cov_in.at[pl.ds(0, n_cand - 1)]
    pltpu.make_async_copy(some, some, c_recv).wait()
    best = cover[...]
    for k in range(n_cand):
        best = jnp.maximum(best, cov_in[k])
    ncov_ref[...] = best

    some = top_in.at[pl.ds(0, n_cand - 1)]
    pltpu.make_async_copy(some, some, t_recv).wait()
    left = lax.broadcasted_iota(jnp.int32, (1, LANES), 1) < TOPK
    for k in range(8):
        rows[k:k + 1, :] = jnp.where(left, top_in[2 * k], top_in[2 * k + 1])
    top_ref[...] = best_sorted(rows, col)[:, :TOPK]

    some = part_in.at[pl.ds(0, n_pts - 1)]
    pltpu.make_async_copy(some, some, p_send).wait()
    some = cov_in.at[pl.ds(0, n_cand - 1)]
    pltpu.make_async_copy(some, some, c_send).wait()
    some = top_in.at[pl.ds(0, n_cand - 1)]
    pltpu.make_async_copy(some, some, t_send).wait()


def on_device(points, weights, coverage, candidates, picks):
    n_pts, n_cand = lax.axis_size("pts"), lax.axis_size("cand")
    n, d = points.shape
    m = candidates.shape[0]
    hbm = pl.BlockSpec(memory_space=pl.ANY)
    vmem = pl.BlockSpec(memory_space=pltpu.VMEM)
    dma = pltpu.SemaphoreType.DMA
    gains, top, ncov = pl.pallas_call(
        functools.partial(kernel, n_pts, n_cand),
        out_shape=(
            jax.ShapeDtypeStruct((8, LANES), F32),
            jax.ShapeDtypeStruct((1, TOPK), F32),
            jax.ShapeDtypeStruct((8, LANES), F32),
        ),
        in_specs=[hbm] * 5,
        out_specs=(vmem, vmem, vmem),
        scratch_shapes=[
            pltpu.VMEM((n, d), jnp.bfloat16),
            pltpu.VMEM((m, d), jnp.bfloat16),
            pltpu.VMEM((8, LANES), F32),
            pltpu.VMEM((8, LANES), F32),
            pltpu.SMEM((TOPK,), jnp.int32),
            pltpu.VMEM((n, LANES), F32),
            pltpu.VMEM((n, LANES), F32),
            pltpu.VMEM((8, LANES), F32),
            pltpu.VMEM((n, LANES), F32),
            pltpu.VMEM((8, 256), F32),
            pltpu.VMEM((1024, LANES), F32),
            pltpu.VMEM((8, LANES), F32),
            pltpu.VMEM((n_pts, 8, LANES), F32),
            pltpu.VMEM((8, LANES), F32),
            pltpu.VMEM((n_cand, 8, LANES), F32),
            pltpu.VMEM((1, LANES), F32),
            pltpu.VMEM((n_cand, 1, LANES), F32),
            pltpu.VMEM((8, LANES), F32),
            dma((6,)), dma, dma, dma, dma, dma, dma,
        ],
        compiler_params=pltpu.CompilerParams(collective_id=0, has_side_effects=True, vmem_limit_bytes=60 * 2**20),
        name="facility",
    )(points, weights.reshape(8, LANES), coverage.reshape(8, LANES), candidates, picks)
    return gains.reshape(m), top.reshape(TOPK), ncov.reshape(n)


def solution(mesh):
    placed = (P("pts", None), P("pts"), P("pts"), P("cand", None), P())
    return jax.shard_map(
        on_device, mesh=mesh, in_specs=placed, out_specs=(P("cand"), P(), P("pts")), check_vma=False
    )
```

time: 70.6 us -> 35.7 us (0.51)
  blocking collectives: 42.1 us -> 0 us
  Pallas kernels: 0 us -> 31.1 us
  other arithmetic: 16.8 us -> 0 us
  matrix products: 4.35 us -> 0 us
  starting transfers between devices: 3.5 us -> 0 us
  local copies, waits for them, and re-layouts: 2.06 us -> 3.7 us
    all_to_all x2 -> x0, blocking collectives: 42.1 us -> none  [from_everyone(): return lax.all_to_all(copies, axis, split_axis=0, concat_axis=0, tiled=True)]
    pallas_call x0 -> x1, Pallas kernels: none -> 31.1 us  [on_device(): pl.pallas_call(functools.partial(kernel, n_pts, n_cand), out_shape=(jax.S...]
    top_k x5 -> x0, other arithmetic: 14.9 us -> none  [the longest x4 10.4 us: best_values(): return lax.top_k(jnp.concatenate([first, second]), TOPK)[0]]
    dot_general x1 -> x0, matrix products: 4.35 us -> none  [on_device(): jnp.dot(points, candidates.T, preferred_element_type=jnp.float32) * scale]
    all_to_all x1 -> x0, starting transfers between devices: 3.5 us -> none  [from_everyone(): return lax.all_to_all(copies, axis, split_axis=0, concat_axis=0, tiled=True)]
    unnamed x6 -> x3, local copies, waits for them, and re-layouts: 0.68 us -> 3.7 us
    reduce_or x1 -> x0, other arithmetic: 0.92 us -> none  [on_device(): chosen = jnp.any(picks[:, None] == columns[None, :], axis=0)]
    broadcast_in_dim x3 -> x0, local copies, waits for them, and re-layouts: 0.73 us -> none  [from_everyone(): copies = jnp.broadcast_to(x, (lax.axis_size(axis), *x.shape))]
  transfers between devices with their start and end apart: 1 -> 0, of which waited for: 1 -> 0; matrix products, arithmetic and copies ran while one was open for 16% -> 0% of each run, Pallas kernels for 0% -> 0%
where the time goes in v1:
time: 35.7 us; the launch traced here: 35.5 us
  Pallas kernels  31.1 us (87%)
  local copies, waits for them, and re-layouts  3.7 us (10%)
  between operations  0.64 us (2%)
    pallas_call x1, Pallas kernels, on_device(): pl.pallas_call(functools.partial(kernel, n_pts, n_cand), out_shape=(jax.S...  31.1 us
    unnamed x3, local copies, waits for them, and re-layouts  3.7 us

profile of v1, /device:TPU:1, one launch (start us, length us, event | category | flops | bytes accessed | tf_op | source)
XLA Modules:
  0.0 35.5 jit_solution(3458404453868019292)
XLA Ops:
  0.6 31.1 %facility.1 = (f32[8,128]{1,0:T(8,128)}, f32[1,64]{1,0:T(1,128)}, f32[8,128]{1,0:T(8,128)}) custom-call(bf16[1024,1024]{1,0:T(8,128)(2,1)} %points_hbm.1, f32[8,128]{1,0:T(8,128)} %bitcast.7, f32[8,128]{1,0:T(8,128)} %bitcast.8, bf16[1024,1024]{1,0:T(8,128)(2,1)} %cand_hbm.1, s32[64]{0:T(128)} %picks_hbm.1), custom_call_target="tpu_custom_call" | custom-call | tf_op jit(solution)/shard_map/facility/pallas_call | solution.py:181
  31.8 1.3 %copy.11 = f32[1024]{0:T(1024)} copy(f32[1024]{0:T(1024)} %bitcast.6) | data formatting | bytes 8192
  33.0 1.2 %copy.12 = f32[64]{0:T(128)} copy(f32[64]{0:T(128)} %bitcast.9) | data formatting | bytes 512
  34.2 1.3 %copy.13 = f32[1024]{0:T(1024)} copy(f32[1024]{0:T(1024)} %bitcast.5) | data formatting | bytes 8192

commit v2 on v1

v2 whole, which is shorter than its diff:
```python
import functools

import jax
import jax.numpy as jnp
from jax import lax
from jax.experimental import pallas as pl
from jax.experimental.pallas import tpu as pltpu
from jax.sharding import PartitionSpec as P

TOPK = 64
LANES = 128
F32 = jnp.float32
VMEM_BYTES = 56557568 - 70 * 1024


def column_of(row):
    return jnp.broadcast_to(row, (LANES, LANES)).T


def descending(rows):
    rows, n, p = list(rows), len(rows), 1
    while p < n:
        k = p
        while k >= 1:
            for j in range(k % p, n - k, 2 * k):
                for i in range(min(k, n - j - k)):
                    if (i + j) // (2 * p) == (i + j + k) // (2 * p):
                        x, y = rows[i + j], rows[i + j + k]
                        rows[i + j], rows[i + j + k] = jnp.maximum(x, y), jnp.minimum(x, y)
            k //= 2
        p *= 2
    return rows


def wide(row):
    return jnp.broadcast_to(row, (8, LANES))


def number_above(columns, row):
    total = jnp.zeros((8, LANES), F32)
    for column in columns:
        total = total + jnp.where(column > row, 1.0, 0.0)
    return wide(jnp.sum(total, axis=0, keepdims=True))


def placed(pairs, blocks, sub):
    result = []
    for block in range(blocks):
        place = sub + float(block * 8)
        best = jnp.full((8, LANES), jnp.inf, F32)
        for row, above in pairs:
            best = jnp.minimum(best, jnp.where(above <= place, row, jnp.inf))
        result.append(jnp.broadcast_to(jnp.min(best, axis=1, keepdims=True), (8, LANES)))
    return result


def as_row(blocks, sub, lane):
    total = jnp.zeros((8, LANES), F32)
    for index, block in enumerate(blocks):
        total = total + jnp.where(lane == sub + float(index * 8), block, 0.0)
    return jnp.sum(total, axis=0, keepdims=True)


def positions():
    sub = lax.broadcasted_iota(jnp.int32, (8, LANES), 0).astype(F32)
    lane = lax.broadcasted_iota(jnp.int32, (8, LANES), 1)
    return sub, lane.astype(F32), lax.rem(lane, TOPK).astype(F32)


def order_pair(rows, columns):
    sub, _, twice = positions()
    pairs = [(wide(row), number_above(columns, wide(row))) for row in rows]
    return as_row(placed(pairs, TOPK // 8, sub), sub, twice)


def best_of_block(total_ref, col_ref):
    sub, lane, _ = positions()
    rows = descending([total_ref[k:k + 1, :] for k in range(8)])
    for k, row in enumerate(rows):
        col_ref[k * LANES:(k + 1) * LANES, :] = column_of(row)
    kept = []
    for k, row in enumerate(rows):
        columns = [col_ref[k * LANES + 8 * j:k * LANES + 8 * j + 8, :] for j in range(16)]
        above = number_above(columns, wide(row))
        kept += placed([(wide(row), above)], -(-(TOPK // (k + 1)) // 8), sub)
    first = as_row(kept[:16], sub, lane)
    second = jnp.where(lane[:1] < 8.0 * (len(kept) - 16), as_row(kept[16:], sub, lane), -jnp.inf)
    return order_pair([first, second], kept)


def best_of_lists(lists, col_ref):
    lane = lax.broadcasted_iota(jnp.int32, (1, LANES), 1)
    rows = descending(lists)
    low = jnp.full((1, LANES), -jnp.inf, F32)
    packed = []
    for group in ((0, 1, 2, 5), (3, 4) + tuple(range(6, len(rows)))):
        at, line = 0, low
        for s in group:
            count = TOPK // (s + 1)
            moved = rows[s] if at % TOPK == 0 else pltpu.roll(rows[s], at, 1)
            line = jnp.where((lane >= at) & (lane < at + count), moved, line)
            at += count
        packed.append((line, at))
    columns = []
    for k, (line, used) in enumerate(packed):
        col_ref[k * LANES:(k + 1) * LANES, :] = column_of(line)
        columns += [col_ref[k * LANES + 8 * j:k * LANES + 8 * j + 8, :] for j in range(-(-used // 8))]
    return order_pair([line for line, _ in packed], columns)


def kernel(n_pts, n_cand, points_hbm, weights_hbm, cover_hbm, cand_hbm, picks_hbm, *refs):
    gains_refs, ncov_refs, top_ref = refs[:8], refs[8:16], refs[16]
    (
        points, cands, weights, cover, picks, wcol, ccol, bias, maxes, col,
        part_out, part_in, cov_out, cov_in, top_out, top_in, gains,
        in_sem, p_send, p_recv, c_send, c_recv, t_send, t_recv, near_sem,
    ) = refs[17:]
    n = points.shape[0]
    m = cands.shape[0]
    me_p = lax.axis_index("pts")
    me_c = lax.axis_index("cand")

    copies = [
        pltpu.make_async_copy(cover_hbm, cover, in_sem.at[0]),
        pltpu.make_async_copy(weights_hbm, weights, in_sem.at[1]),
        pltpu.make_async_copy(picks_hbm, picks, in_sem.at[2]),
        pltpu.make_async_copy(cand_hbm.at[pl.ds(0, 256)], cands.at[pl.ds(0, 256)], in_sem.at[3]),
        pltpu.make_async_copy(points_hbm, points, in_sem.at[4]),
        pltpu.make_async_copy(cand_hbm.at[pl.ds(256, 768)], cands.at[pl.ds(256, 768)], in_sem.at[5]),
    ]
    for copy in copies:
        copy.start()

    barrier = pltpu.get_barrier_semaphore()
    for k in range(1, n_pts):
        pl.semaphore_signal(barrier, 1, device_id={"pts": lax.rem(me_p + k, n_pts)}, device_id_type=pl.DeviceIdType.MESH)
    for k in (1, n_cand - 1):
        pl.semaphore_signal(barrier, 1, device_id={"cand": lax.rem(me_c + k, n_cand)}, device_id_type=pl.DeviceIdType.MESH)

    copies[0].wait()
    copies[1].wait()
    for k in range(8):
        ccol[k * LANES:(k + 1) * LANES, :] = column_of(cover[k:k + 1, :] * 32.0)
        wcol[k * LANES:(k + 1) * LANES, :] = column_of(weights[k:k + 1, :] * (2.0 ** -20))
    copies[2].wait()
    column = (
        me_c * m
        + lax.broadcasted_iota(jnp.int32, (8, LANES), 0) * LANES
        + lax.broadcasted_iota(jnp.int32, (8, LANES), 1)
    )
    mask = jnp.full((8, LANES), -1e30, F32)
    for k in range(TOPK):
        mask = jnp.where(column == picks[k], 0.0, mask)
    bias[...] = mask
    copies[3].wait()
    copies[4].wait()

    block = 256
    for tile in range(4):
        if tile == 1:
            copies[5].wait()
        rhs = cands[tile * 256:(tile + 1) * 256, :]
        halves = [bias[2 * tile + h:2 * tile + h + 1, :] for h in range(2)]
        sums = [jnp.zeros((8, LANES), F32) for _ in range(2)]
        for b in range(n // block):
            at = slice(b * block, (b + 1) * block)
            sims = lax.dot_general(
                points[at, :], rhs, (((1,), (1,)), ((), ())), preferred_element_type=F32
            )
            high = None
            for h in range(2):
                s = sims[:, h * LANES:(h + 1) * LANES]
                t = jnp.maximum(s - ccol[at, :], 0.0) * wcol[at, :]
                sums[h] = sums[h] + jnp.sum(t.reshape(block // 8, 8, LANES), axis=0)
                masked = s + halves[h]
                high = masked if high is None else jnp.maximum(high, masked)
            if tile == 0:
                maxes[at, :] = high
            else:
                maxes[at, :] = jnp.maximum(maxes[at, :], high)
        for h in range(2):
            part_out[2 * tile + h:2 * tile + h + 1, :] = jnp.sum(sums[h], axis=0, keepdims=True)

    pl.semaphore_wait(barrier, n_pts + 1)
    part_in[me_p] = part_out[...]
    for k in range(1, n_pts):
        pltpu.make_async_remote_copy(
            part_out, part_in.at[me_p], p_send, p_recv,
            device_id={"pts": lax.rem(me_p + k, n_pts)}, device_id_type=pl.DeviceIdType.MESH,
        ).start()
    reach, rounds = 1, 0
    while reach < n_cand // 2:
        for k in (reach, n_cand - reach):
            pl.semaphore_signal(
                near_sem.at[rounds], 1, device_id={"cand": lax.rem(me_c + k, n_cand)}, device_id_type=pl.DeviceIdType.MESH
            )
        if rounds == 0:
            for k in range(8):
                high = maxes[k * LANES:(k + 1) * LANES, :].T
                cov_out[k:k + 1, :] = jnp.max(high, axis=0, keepdims=True) * (2.0 ** -5)
        pl.semaphore_wait(near_sem.at[rounds], 2)
        reach, rounds = 2 * reach, rounds + 1
    for k in range(1, n_cand):
        pltpu.make_async_remote_copy(
            cov_out, cov_in.at[k], c_send, c_recv,
            device_id={"cand": lax.rem(me_c + k, n_cand)}, device_id_type=pl.DeviceIdType.MESH,
        ).start()

    some = part_in.at[pl.ds(0, n_pts - 1)]
    pltpu.make_async_copy(some, some, p_recv).wait()
    total = part_in[0]
    for k in range(1, n_pts):
        total = total + part_in[k]
    gains[...] = total
    top_out[...] = best_of_block(gains, col)
    for k in range(1, n_cand):
        pltpu.make_async_remote_copy(
            top_out, top_in.at[k], t_send, t_recv,
            device_id={"cand": lax.rem(me_c + k, n_cand)}, device_id_type=pl.DeviceIdType.MESH,
        ).start()

    some = cov_in.at[pl.ds(1, n_cand - 1)]
    pltpu.make_async_copy(some, some, c_recv).wait()
    best = jnp.maximum(cover[...], cov_out[...])
    for k in range(1, n_cand):
        best = jnp.maximum(best, cov_in[k])
    for k in range(8):
        gains_refs[k][...] = gains[k:k + 1, :]
        ncov_refs[k][...] = best[k:k + 1, :]

    for sent, sem, count in ((part_in, p_send, n_pts - 1), (cov_in, c_send, n_cand - 1), (top_in, t_send, n_cand - 1)):
        some = sent.at[pl.ds(0, count)]
        pltpu.make_async_copy(some, some, sem).wait()

    some = top_in.at[pl.ds(1, n_cand - 1)]
    pltpu.make_async_copy(some, some, t_recv).wait()
    best = best_of_lists([top_out[...]] + [top_in[k] for k in range(1, n_cand)], col)
    top_ref[...] = best


def write_out(*refs):
    rows, (gains, ncov, top), (best, sem) = refs[:17], refs[17:20], refs[20:]
    best[...] = rows[16][:, :TOPK]
    copies = [pltpu.make_async_copy(best, top, sem.at[16])]
    for k in range(8):
        copies.append(pltpu.make_async_copy(rows[k], gains.at[pl.ds(k, 1)], sem.at[k]))
        copies.append(pltpu.make_async_copy(rows[8 + k], ncov.at[pl.ds(k, 1)], sem.at[8 + k]))
    for copy in copies:
        copy.start()
    for copy in copies:
        copy.wait()


def on_device(points, weights, coverage, candidates, picks):
    n_pts, n_cand = lax.axis_size("pts"), lax.axis_size("cand")
    n, d = points.shape
    m = candidates.shape[0]
    hbm = pl.BlockSpec(memory_space=pl.ANY)
    vmem = pl.BlockSpec(memory_space=pltpu.VMEM)
    dma = pltpu.SemaphoreType.DMA
    inside = pl.pallas_call(
        functools.partial(kernel, n_pts, n_cand),
        out_shape=(jax.ShapeDtypeStruct((1, LANES), F32),) * 17,
        in_specs=[hbm] * 5,
        out_specs=(vmem,) * 17,
        scratch_shapes=[
            pltpu.VMEM((n, d), jnp.bfloat16),
            pltpu.VMEM((m, d), jnp.bfloat16),
            pltpu.VMEM((8, LANES), F32),
            pltpu.VMEM((8, LANES), F32),
            pltpu.SMEM((TOPK,), jnp.int32),
            pltpu.VMEM((n, LANES), F32),
            pltpu.VMEM((n, LANES), F32),
            pltpu.VMEM((8, LANES), F32),
            pltpu.VMEM((n, LANES), F32),
            pltpu.VMEM((1024, LANES), F32),
            pltpu.VMEM((8, LANES), F32),
            pltpu.VMEM((n_pts, 8, LANES), F32),
            pltpu.VMEM((8, LANES), F32),
            pltpu.VMEM((n_cand, 8, LANES), F32),
            pltpu.VMEM((1, LANES), F32),
            pltpu.VMEM((n_cand, 1, LANES), F32),
            pltpu.VMEM((8, LANES), F32),
            dma((6,)), dma, dma, dma, dma, dma, dma, pltpu.SemaphoreType.REGULAR((3,)),
        ],
        compiler_params=pltpu.CompilerParams(
            collective_id=0, has_side_effects=True, vmem_limit_bytes=VMEM_BYTES
        ),
        name="facility",
    )(points, weights.reshape(8, LANES), coverage.reshape(8, LANES), candidates, picks)
    gains, ncov, top = pl.pallas_call(
        write_out,
        out_shape=(
            jax.ShapeDtypeStruct((8, LANES), F32),
            jax.ShapeDtypeStruct((8, LANES), F32),
            jax.ShapeDtypeStruct((1, TOPK), F32),
        ),
        in_specs=[vmem] * 17,
        out_specs=(hbm, hbm, hbm),
        scratch_shapes=[pltpu.VMEM((1, TOPK), F32), dma((17,))],
        compiler_params=pltpu.CompilerParams(vmem_limit_bytes=2**20),
        name="write_out",
    )(*inside)
    return gains.reshape(m), top.reshape(TOPK), ncov.reshape(n)


def solution(mesh):
    placed = (P("pts", None), P("pts"), P("pts"), P("cand", None), P())
    return jax.shard_map(
        on_device, mesh=mesh, in_specs=placed, out_specs=(P("cand"), P(), P("pts")), check_vma=False
    )
```

time: 35.7 us -> 31.4 us (0.88)
  local copies, waits for them, and re-layouts: 3.7 us -> 0 us
  Pallas kernels: 31.1 us -> 30.6 us
    unnamed x3 -> x0, local copies, waits for them, and re-layouts: 3.7 us -> none
    pallas_call x1, Pallas kernels: 31.1 us -> 29.9 us  [on_device(): pl.pallas_call(functools.partial(kernel, n_pts, n_cand), out_shape=(jax.S...]
    pallas_call x0 -> x1, Pallas kernels: none -> 0.73 us  [on_device(): pl.pallas_call(write_out, out_shape=(jax.ShapeDtypeStruct((8, LANES), F32...]
where the time goes in v2:
time: 31.4 us; the launch traced here: 31.3 us
  Pallas kernels  30.6 us (97%)
  between operations  0.64 us (2%)
    pallas_call x1, Pallas kernels, on_device(): pl.pallas_call(functools.partial(kernel, n_pts, n_cand), out_shape=(jax.S...  29.9 us
    pallas_call x1, Pallas kernels, on_device(): pl.pallas_call(write_out, out_shape=(jax.ShapeDtypeStruct((8, LANES), F32...  0.73 us

profile of v2, /device:TPU:1, one launch (start us, length us, event | category | flops | bytes accessed | tf_op | source)
XLA Modules:
  0.0 31.3 jit_solution(4892373484392641020)
XLA Ops:
  0.6 29.9 %facility.1 = (f32[1,128]{1,0:T(1,128)S(1)}, f32[1,128]{1,0:T(1,128)S(1)}, f32[1,128]{1,0:T(1,128)S(1)}, f32[1,128]{1,0:T(1,128)S(1)}, f32[1,128]{1,0:T(1,128)S(...) custom-call(bf16[1024,1024]{1,0:T(8,128)(2,1)} %points_hbm.1, ...), custom_call_target="tpu_custom_call" | custom-call | tf_op jit(solution)/shard_map/facility/pallas_call | solution.py:261
  30.5 0.7 %write_out.1 = (f32[8,128]{1,0:T(8,128)}, f32[8,128]{1,0:T(8,128)}, f32[1,64]{1,0:T(1,128)}) custom-call(f32[1,128]{1,0:T(1,128)S(1)} %get-tuple-element.23.refs_0_, f32[1,128]{1,0:T(1,128)S(1)} %get-tuple-element.24.refs_1_, f32[1,128]{1,0:T(1,128)S(1)} %get-tuple-element.25.refs_2_, f32[1,128]{1,0:T(1,128)S(1)} %get-tuple-element.26.refs_3_, ...), custom_call_target="tpu_custom_call" | custom-call | tf_op jit(solution)/shard_map/write_out/pallas_call | solution.py:291

commit v3 on v2

--- a/solution.py
+++ b/solution.py
@@ -120,21 +120,31 @@
     me_p = lax.axis_index("pts")
     me_c = lax.axis_index("cand")
 
+    half = n // 2
+    place = [lax.rem(me_p // 8 + k, 4) * 8 for k in range(4)], [lax.rem(me_p // 2 + k, 4) * 2 for k in range(4)]
+    cores = lax.rem(me_p, 2), 1 - lax.rem(me_p, 2)
+    offsets = [(x, y, c) for x in range(4) for y in range(4) for c in range(2) if x or y or c]
+    offsets.sort(key=lambda o: -(min(o[0], 4 - o[0]) + min(o[1], 4 - o[1])))
+    far_first = [place[0][x] + place[1][y] + cores[c] for x, y, c in offsets]
+    along = sorted(range(1, n_cand), key=lambda k: -min(k, n_cand - k))
     copies = [
         pltpu.make_async_copy(cover_hbm, cover, in_sem.at[0]),
         pltpu.make_async_copy(weights_hbm, weights, in_sem.at[1]),
         pltpu.make_async_copy(picks_hbm, picks, in_sem.at[2]),
-        pltpu.make_async_copy(cand_hbm.at[pl.ds(0, 256)], cands.at[pl.ds(0, 256)], in_sem.at[3]),
-        pltpu.make_async_copy(points_hbm, points, in_sem.at[4]),
-        pltpu.make_async_copy(cand_hbm.at[pl.ds(256, 768)], cands.at[pl.ds(256, 768)], in_sem.at[5]),
+        pltpu.make_async_copy(cand_hbm.at[pl.ds(0, m // 2)], cands.at[pl.ds(0, m // 2)], in_sem.at[3]),
+        pltpu.make_async_copy(points_hbm.at[pl.ds(0, half)], points.at[pl.ds(0, half)], in_sem.at[4]),
+        pltpu.make_async_copy(points_hbm.at[pl.ds(half, half)], points.at[pl.ds(half, half)], in_sem.at[5]),
+        pltpu.make_async_copy(cand_hbm.at[pl.ds(m // 2, m // 2)], cands.at[pl.ds(m // 2, m // 2)], in_sem.at[6]),
     ]
     for copy in copies:
         copy.start()
 
+    near = 4
+    beside = [k for k in range(1, n_cand) if min(k, n_cand - k) <= near]
     barrier = pltpu.get_barrier_semaphore()
-    for k in range(1, n_pts):
-        pl.semaphore_signal(barrier, 1, device_id={"pts": lax.rem(me_p + k, n_pts)}, device_id_type=pl.DeviceIdType.MESH)
-    for k in (1, n_cand - 1):
+    for peer in far_first:
+        pl.semaphore_signal(barrier, 1, device_id={"pts": peer}, device_id_type=pl.DeviceIdType.MESH)
+    for k in beside:
         pl.semaphore_signal(barrier, 1, device_id={"cand": lax.rem(me_c + k, n_cand)}, device_id_type=pl.DeviceIdType.MESH)
 
     copies[0].wait()
@@ -155,40 +165,44 @@
     copies[3].wait()
     copies[4].wait()
 
-    block = 256
-    for tile in range(4):
-        if tile == 1:
-            copies[5].wait()
-        rhs = cands[tile * 256:(tile + 1) * 256, :]
-        halves = [bias[2 * tile + h:2 * tile + h + 1, :] for h in range(2)]
-        sums = [jnp.zeros((8, LANES), F32) for _ in range(2)]
-        for b in range(n // block):
-            at = slice(b * block, (b + 1) * block)
-            sims = lax.dot_general(
-                points[at, :], rhs, (((1,), (1,)), ((), ())), preferred_element_type=F32
-            )
-            high = None
-            for h in range(2):
-                s = sims[:, h * LANES:(h + 1) * LANES]
-                t = jnp.maximum(s - ccol[at, :], 0.0) * wcol[at, :]
-                sums[h] = sums[h] + jnp.sum(t.reshape(block // 8, 8, LANES), axis=0)
-                masked = s + halves[h]
-                high = masked if high is None else jnp.maximum(high, masked)
-            if tile == 0:
-                maxes[at, :] = high
-            else:
-                maxes[at, :] = jnp.maximum(maxes[at, :], high)
+    sums = [jnp.zeros((8, LANES), F32) for _ in range(8)]
+
+    def multiply(tile, rows, first):
+        at = slice(rows * half, (rows + 1) * half)
+        sims = lax.dot_general(
+            points[at, :], cands[tile * 256:(tile + 1) * 256, :], (((1,), (1,)), ((), ())), preferred_element_type=F32
+        )
+        high = None
         for h in range(2):
-            part_out[2 * tile + h:2 * tile + h + 1, :] = jnp.sum(sums[h], axis=0, keepdims=True)
-
-    pl.semaphore_wait(barrier, n_pts + 1)
-    part_in[me_p] = part_out[...]
-    for k in range(1, n_pts):
-        pltpu.make_async_remote_copy(
-            part_out, part_in.at[me_p], p_send, p_recv,
-            device_id={"pts": lax.rem(me_p + k, n_pts)}, device_id_type=pl.DeviceIdType.MESH,
-        ).start()
-    reach, rounds = 1, 0
+            s = sims[:, h * LANES:(h + 1) * LANES]
+            t = jnp.maximum(s - ccol[at, :], 0.0) * wcol[at, :]
+            sums[2 * tile + h] = sums[2 * tile + h] + jnp.sum(t.reshape(half // 8, 8, LANES), axis=0)
+            masked = s + bias[2 * tile + h:2 * tile + h + 1, :]
+            high = masked if high is None else jnp.maximum(high, masked)
+        maxes[at, :] = high if first else jnp.maximum(maxes[at, :], high)
+
+    def send_parts(start, size):
+        for k in range(start, start + size):
+            part_out[k:k + 1, :] = jnp.sum(sums[k], axis=0, keepdims=True)
+        part_in[me_p, start:start + size, :] = part_out[start:start + size, :]
+        for peer in far_first:
+            pltpu.make_async_remote_copy(
+                part_out.at[pl.ds(start, size)], part_in.at[me_p, pl.ds(start, size)], p_send, p_recv,
+                device_id={"pts": peer}, device_id_type=pl.DeviceIdType.MESH,
+            ).start()
+
+    multiply(0, 0, True)
+    multiply(1, 0, False)
+    copies[5].wait()
+    copies[6].wait()
+    multiply(0, 1, True)
+    multiply(1, 1, False)
+    for tile in (2, 3):
+        for rows in (0, 1):
+            multiply(tile, rows, False)
+    pl.semaphore_wait(barrier, n_pts - 1 + len(beside))
+    send_parts(0, 8)
+    reach, rounds = near, 0
     while reach < n_cand // 2:
         for k in (reach, n_cand - reach):
             pl.semaphore_signal(
@@ -200,7 +214,7 @@
                 cov_out[k:k + 1, :] = jnp.max(high, axis=0, keepdims=True) * (2.0 ** -5)
         pl.semaphore_wait(near_sem.at[rounds], 2)
         reach, rounds = 2 * reach, rounds + 1
-    for k in range(1, n_cand):
+    for k in along:
         pltpu.make_async_remote_copy(
             cov_out, cov_in.at[k], c_send, c_recv,
             device_id={"cand": lax.rem(me_c + k, n_cand)}, device_id_type=pl.DeviceIdType.MESH,
@@ -213,7 +227,7 @@
         total = total + part_in[k]
     gains[...] = total
     top_out[...] = best_of_block(gains, col)
-    for k in range(1, n_cand):
+    for k in along:
         pltpu.make_async_remote_copy(
             top_out, top_in.at[k], t_send, t_recv,
             device_id={"cand": lax.rem(me_c + k, n_cand)}, device_id_type=pl.DeviceIdType.MESH,
@@ -281,7 +295,7 @@
             pltpu.VMEM((1, LANES), F32),
             pltpu.VMEM((n_cand, 1, LANES), F32),
             pltpu.VMEM((8, LANES), F32),
-            dma((6,)), dma, dma, dma, dma, dma, dma, pltpu.SemaphoreType.REGULAR((3,)),
+            dma((7,)), dma, dma, dma, dma, dma, dma, pltpu.SemaphoreType.REGULAR((1,)),
         ],
         compiler_params=pltpu.CompilerParams(
             collective_id=0, has_side_effects=True, vmem_limit_bytes=VMEM_BYTES

time: 31.4 us -> 30.4 us (0.968)
  Pallas kernels: 30.6 us -> 29.6 us
    pallas_call x1, Pallas kernels: 29.9 us -> 28.9 us  [on_device(): pl.pallas_call(functools.partial(kernel, n_pts, n_cand), out_shape=(jax.S...]
where the time goes in v3:
time: 30.4 us; the launch traced here: 30.3 us
  Pallas kernels  29.6 us (97%)
  between operations  0.64 us (2%)
    pallas_call x1, Pallas kernels, on_device(): pl.pallas_call(functools.partial(kernel, n_pts, n_cand), out_shape=(jax.S...  28.9 us
    pallas_call x1, Pallas kernels, on_device(): pl.pallas_call(write_out, out_shape=(jax.ShapeDtypeStruct((8, LANES), F32...  0.73 us

profile of v3, /device:TPU:1, one launch (start us, length us, event | category | flops | bytes accessed | tf_op | source)
XLA Modules:
  0.0 30.3 jit_solution(18011528426356953861)
XLA Ops:
  0.6 28.9 %facility.1 = (f32[1,128]{1,0:T(1,128)S(1)}, f32[1,128]{1,0:T(1,128)S(1)}, f32[1,128]{1,0:T(1,128)S(1)}, f32[1,128]{1,0:T(1,128)S(1)}, f32[1,128]{1,0:T(1,128)S(...) custom-call(bf16[1024,1024]{1,0:T(8,128)(2,1)} %points_hbm.1, ...), custom_call_target="tpu_custom_call" | custom-call | tf_op jit(solution)/shard_map/facility/pallas_call | solution.py:275
  29.5 0.7 %write_out.1 = (f32[8,128]{1,0:T(8,128)}, f32[8,128]{1,0:T(8,128)}, f32[1,64]{1,0:T(1,128)}) custom-call(f32[1,128]{1,0:T(1,128)S(1)} %get-tuple-element.23.refs_0_, f32[1,128]{1,0:T(1,128)S(1)} %get-tuple-element.24.refs_1_, f32[1,128]{1,0:T(1,128)S(1)} %get-tuple-element.25.refs_2_, f32[1,128]{1,0:T(1,128)S(1)} %get-tuple-element.26.refs_3_, ...), custom_call_target="tpu_custom_call" | custom-call | tf_op jit(solution)/shard_map/write_out/pallas_call | solution.py:305

commit v4 on v3

--- a/solution.py
+++ b/solution.py
@@ -36,10 +36,14 @@
     return jnp.broadcast_to(row, (8, LANES))
 
 
+def added(terms):
+    while len(terms) > 1:
+        terms = [x + y for x, y in zip(terms[::2], terms[1::2])] + ([terms[-1]] if len(terms) % 2 else [])
+    return terms[0]
+
+
 def number_above(columns, row):
-    total = jnp.zeros((8, LANES), F32)
-    for column in columns:
-        total = total + jnp.where(column > row, 1.0, 0.0)
+    total = added([jnp.where(column > row, 1.0, 0.0) for column in columns])
     return wide(jnp.sum(total, axis=0, keepdims=True))
 
 
@@ -55,9 +59,7 @@
 
 
 def as_row(blocks, sub, lane):
-    total = jnp.zeros((8, LANES), F32)
-    for index, block in enumerate(blocks):
-        total = total + jnp.where(lane == sub + float(index * 8), block, 0.0)
+    total = added([jnp.where(lane == sub + float(index * 8), block, 0.0) for index, block in enumerate(blocks)])
     return jnp.sum(total, axis=0, keepdims=True)
 
 
@@ -96,11 +98,13 @@
     for group in ((0, 1, 2, 5), (3, 4) + tuple(range(6, len(rows)))):
         at, line = 0, low
         for s in group:
-            count = TOPK // (s + 1)
-            moved = rows[s] if at % TOPK == 0 else pltpu.roll(rows[s], at, 1)
-            line = jnp.where((lane >= at) & (lane < at + count), moved, line)
-            at += count
-        packed.append((line, at))
+            if s < len(rows):
+                count = TOPK // (s + 1)
+                moved = rows[s] if at % TOPK == 0 else pltpu.roll(rows[s], at, 1)
+                line = jnp.where((lane >= at) & (lane < at + count), moved, line)
+                at += count
+        if at:
+            packed.append((line, at))
     columns = []
     for k, (line, used) in enumerate(packed):
         col_ref[k * LANES:(k + 1) * LANES, :] = column_of(line)
@@ -126,6 +130,7 @@
     offsets = [(x, y, c) for x in range(4) for y in range(4) for c in range(2) if x or y or c]
     offsets.sort(key=lambda o: -(min(o[0], 4 - o[0]) + min(o[1], 4 - o[1])))
     far_first = [place[0][x] + place[1][y] + cores[c] for x, y, c in offsets]
+    farthest = n_cand // 2
     along = sorted(range(1, n_cand), key=lambda k: -min(k, n_cand - k))
     copies = [
         pltpu.make_async_copy(cover_hbm, cover, in_sem.at[0]),
@@ -229,7 +234,7 @@
     top_out[...] = best_of_block(gains, col)
     for k in along:
         pltpu.make_async_remote_copy(
-            top_out, top_in.at[k], t_send, t_recv,
+            top_out, top_in.at[k], t_send, t_recv.at[int(k == farthest)],
             device_id={"cand": lax.rem(me_c + k, n_cand)}, device_id_type=pl.DeviceIdType.MESH,
         ).start()
 
@@ -242,23 +247,30 @@
         gains_refs[k][...] = gains[k:k + 1, :]
         ncov_refs[k][...] = best[k:k + 1, :]
 
+    some = top_in.at[pl.ds(0, n_cand - 2)]
+    pltpu.make_async_copy(some, some, t_recv.at[0]).wait()
+    best = best_of_lists([top_out[...]] + [top_in[k] for k in range(1, n_cand) if k != farthest], col)
+
     for sent, sem, count in ((part_in, p_send, n_pts - 1), (cov_in, c_send, n_cand - 1), (top_in, t_send, n_cand - 1)):
         some = sent.at[pl.ds(0, count)]
         pltpu.make_async_copy(some, some, sem).wait()
 
-    some = top_in.at[pl.ds(1, n_cand - 1)]
-    pltpu.make_async_copy(some, some, t_recv).wait()
-    best = best_of_lists([top_out[...]] + [top_in[k] for k in range(1, n_cand)], col)
-    top_ref[...] = best
+    some = top_in.at[pl.ds(farthest, 1)]
+    pltpu.make_async_copy(some, some, t_recv.at[1]).wait()
+    top_ref[...] = best_of_lists([best, top_in[farthest]], col)
 
 
 def write_out(*refs):
-    rows, (gains, ncov, top), (best, sem) = refs[:17], refs[17:20], refs[20:]
+    rows, (gains, ncov, top), (gains_all, ncov_all, best, sem) = refs[:17], refs[17:20], refs[20:]
     best[...] = rows[16][:, :TOPK]
-    copies = [pltpu.make_async_copy(best, top, sem.at[16])]
     for k in range(8):
-        copies.append(pltpu.make_async_copy(rows[k], gains.at[pl.ds(k, 1)], sem.at[k]))
-        copies.append(pltpu.make_async_copy(rows[8 + k], ncov.at[pl.ds(k, 1)], sem.at[8 + k]))
+        gains_all[k:k + 1, :] = rows[k][...]
+        ncov_all[k:k + 1, :] = rows[8 + k][...]
+    copies = [
+        pltpu.make_async_copy(best, top, sem.at[0]),
+        pltpu.make_async_copy(gains_all, gains, sem.at[1]),
+        pltpu.make_async_copy(ncov_all, ncov, sem.at[2]),
+    ]
     for copy in copies:
         copy.start()
     for copy in copies:
@@ -295,7 +307,7 @@
             pltpu.VMEM((1, LANES), F32),
             pltpu.VMEM((n_cand, 1, LANES), F32),
             pltpu.VMEM((8, LANES), F32),
-            dma((7,)), dma, dma, dma, dma, dma, dma, pltpu.SemaphoreType.REGULAR((1,)),
+            dma((7,)), dma, dma, dma, dma, dma, dma((2,)), pltpu.SemaphoreType.REGULAR((1,)),
         ],
         compiler_params=pltpu.CompilerParams(
             collective_id=0, has_side_effects=True, vmem_limit_bytes=VMEM_BYTES
@@ -311,7 +323,9 @@
         ),
         in_specs=[vmem] * 17,
         out_specs=(hbm, hbm, hbm),
-        scratch_shapes=[pltpu.VMEM((1, TOPK), F32), dma((17,))],
+        scratch_shapes=[
+            pltpu.VMEM((8, LANES), F32), pltpu.VMEM((8, LANES), F32), pltpu.VMEM((1, TOPK), F32), dma((3,))
+        ],
         compiler_params=pltpu.CompilerParams(vmem_limit_bytes=2**20),
         name="write_out",
     )(*inside)

time: 30.4 us -> 30.2 us (level)
  no operation moved by 1% of the time
where the time goes in v4:
time: 30.2 us; the launch traced here: 30.1 us
  Pallas kernels  29.4 us (97%)
  between operations  0.64 us (2%)
    pallas_call x1, Pallas kernels, on_device(): pl.pallas_call(functools.partial(kernel, n_pts, n_cand), out_shape=(jax.S...  28.8 us
    pallas_call x1, Pallas kernels, on_device(): pl.pallas_call(write_out, out_shape=(jax.ShapeDtypeStruct((8, LANES), F32...  0.64 us

profile of v4, /device:TPU:1, one launch (start us, length us, event | category | flops | bytes accessed | tf_op | source)
XLA Modules:
  0.0 30.1 jit_solution(11253638132000562408)
XLA Ops:
  0.6 28.8 %facility.1 = (f32[1,128]{1,0:T(1,128)S(1)}, f32[1,128]{1,0:T(1,128)S(1)}, f32[1,128]{1,0:T(1,128)S(1)}, f32[1,128]{1,0:T(1,128)S(1)}, f32[1,128]{1,0:T(1,128)S(...) custom-call(bf16[1024,1024]{1,0:T(8,128)(2,1)} %points_hbm.1, ...), custom_call_target="tpu_custom_call" | custom-call | tf_op jit(solution)/shard_map/facility/pallas_call | solution.py:287
  29.4 0.6 %write_out.1 = (f32[8,128]{1,0:T(8,128)}, f32[8,128]{1,0:T(8,128)}, f32[1,64]{1,0:T(1,128)}) custom-call(f32[1,128]{1,0:T(1,128)S(1)} %get-tuple-element.23.refs_0_, f32[1,128]{1,0:T(1,128)S(1)} %get-tuple-element.24.refs_1_, f32[1,128]{1,0:T(1,128)S(1)} %get-tuple-element.25.refs_2_, f32[1,128]{1,0:T(1,128)S(1)} %get-tuple-element.26.refs_3_, ...), custom_call_target="tpu_custom_call" | custom-call | tf_op jit(solution)/shard_map/write_out/pallas_call | solution.py:317

commit v5 on v4

v5 whole, which is shorter than its diff:
```python
import functools

import jax
import jax.numpy as jnp
from jax import lax
from jax.experimental import pallas as pl
from jax.experimental.pallas import tpu as pltpu
from jax.sharding import PartitionSpec as P

TOPK = 64
LANES = 128
F32 = jnp.float32
VMEM_BYTES = 56557568 - 70 * 1024


def column_of(row):
    return jnp.broadcast_to(row, (LANES, LANES)).T


def descending(rows):
    rows, n, p = list(rows), len(rows), 1
    while p < n:
        k = p
        while k >= 1:
            for j in range(k % p, n - k, 2 * k):
                for i in range(min(k, n - j - k)):
                    if (i + j) // (2 * p) == (i + j + k) // (2 * p):
                        x, y = rows[i + j], rows[i + j + k]
                        rows[i + j], rows[i + j + k] = jnp.maximum(x, y), jnp.minimum(x, y)
            k //= 2
        p *= 2
    return rows


def wide(row):
    return jnp.broadcast_to(row, (8, LANES))


def added(terms):
    while len(terms) > 1:
        terms = [x + y for x, y in zip(terms[::2], terms[1::2])] + ([terms[-1]] if len(terms) % 2 else [])
    return terms[0]


def number_above(columns, row):
    total = added([jnp.where(column > row, 1.0, 0.0) for column in columns])
    return wide(jnp.sum(total, axis=0, keepdims=True))


def placed(pairs, blocks, sub):
    result = []
    for block in range(blocks):
        place = sub + float(block * 8)
        best = jnp.full((8, LANES), jnp.inf, F32)
        for row, above in pairs:
            best = jnp.minimum(best, jnp.where(above <= place, row, jnp.inf))
        result.append(jnp.broadcast_to(jnp.min(best, axis=1, keepdims=True), (8, LANES)))
    return result


def as_row(blocks, sub, lane):
    total = added([jnp.where(lane == sub + float(index * 8), block, 0.0) for index, block in enumerate(blocks)])
    return jnp.sum(total, axis=0, keepdims=True)


def positions():
    sub = lax.broadcasted_iota(jnp.int32, (8, LANES), 0).astype(F32)
    lane = lax.broadcasted_iota(jnp.int32, (8, LANES), 1)
    return sub, lane.astype(F32), lax.rem(lane, TOPK).astype(F32)


def order_pair(rows, columns):
    sub, _, twice = positions()
    pairs = [(wide(row), number_above(columns, wide(row))) for row in rows]
    return as_row(placed(pairs, TOPK // 8, sub), sub, twice)


def best_of_block(total_ref, col_ref):
    sub, lane, _ = positions()
    rows = descending([total_ref[k:k + 1, :] for k in range(8)])
    for k, row in enumerate(rows):
        col_ref[k * LANES:(k + 1) * LANES, :] = column_of(row)
    kept = []
    for k, row in enumerate(rows):
        columns = [col_ref[k * LANES + 8 * j:k * LANES + 8 * j + 8, :] for j in range(16)]
        above = number_above(columns, wide(row))
        kept += placed([(wide(row), above)], -(-(TOPK // (k + 1)) // 8), sub)
    first = as_row(kept[:16], sub, lane)
    second = jnp.where(lane[:1] < 8.0 * (len(kept) - 16), as_row(kept[16:], sub, lane), -jnp.inf)
    return order_pair([first, second], kept)


def best_of_lists(lists, col_ref):
    lane = lax.broadcasted_iota(jnp.int32, (1, LANES), 1)
    rows = descending(lists)
    low = jnp.full((1, LANES), -jnp.inf, F32)
    packed = []
    for group in ((0, 1, 2, 5), (3, 4) + tuple(range(6, len(rows)))):
        at, line = 0, low
        for s in group:
            if s < len(rows):
                count = TOPK // (s + 1)
                moved = rows[s] if at % TOPK == 0 else pltpu.roll(rows[s], at, 1)
                line = jnp.where((lane >= at) & (lane < at + count), moved, line)
                at += count
        if at:
            packed.append((line, at))
    columns = []
    for k, (line, used) in enumerate(packed):
        col_ref[k * LANES:(k + 1) * LANES, :] = column_of(line)
        columns += [col_ref[k * LANES + 8 * j:k * LANES + 8 * j + 8, :] for j in range(-(-used // 8))]
    return order_pair([line for line, _ in packed], columns)


def kernel(n_pts, n_cand, points_hbm, weights_hbm, cover_hbm, cand_hbm, picks_hbm, *refs):
    gains_refs, ncov_refs, top_ref = refs[:8], refs[8:16], refs[16]
    (
        points, cands, weights, cover, picks, wcol, ccol, bias, maxes, col,
        part_out, part_in, cov_out, cov_in, top_out, top_in, top_near, gains,
        p_recv, c_recv, t_recv, near_sem,
    ) = refs[17:]
    farthest = n_cand // 2

    def until_last_list(in_sem, p_send, c_send, t_send):
        n = points.shape[0]
        m = cands.shape[0]
        me_p = lax.axis_index("pts")
        me_c = lax.axis_index("cand")

        half = n // 2
        others = [k + lax.div(k - me_p + n_pts - 1, n_pts - 1) for k in range(n_pts - 1)]
        along = sorted(range(1, n_cand), key=lambda k: -min(k, n_cand - k))
        copies = [
            pltpu.make_async_copy(cover_hbm, cover, in_sem.at[0]),
            pltpu.make_async_copy(weights_hbm, weights, in_sem.at[1]),
            pltpu.make_async_copy(picks_hbm, picks, in_sem.at[2]),
            pltpu.make_async_copy(cand_hbm.at[pl.ds(0, m // 2)], cands.at[pl.ds(0, m // 2)], in_sem.at[3]),
            pltpu.make_async_copy(points_hbm.at[pl.ds(0, half)], points.at[pl.ds(0, half)], in_sem.at[4]),
            pltpu.make_async_copy(points_hbm.at[pl.ds(half, half)], points.at[pl.ds(half, half)], in_sem.at[5]),
            pltpu.make_async_copy(cand_hbm.at[pl.ds(m // 2, m // 2)], cands.at[pl.ds(m // 2, m // 2)], in_sem.at[6]),
        ]
        for copy in copies:
            copy.start()

        near = 4
        beside = [k for k in range(1, n_cand) if min(k, n_cand - k) <= near]
        barrier = pltpu.get_barrier_semaphore()
        for peer in others:
            pl.semaphore_signal(barrier, 1, device_id={"pts": peer}, device_id_type=pl.DeviceIdType.MESH)
        for k in beside:
            pl.semaphore_signal(barrier, 1, device_id={"cand": lax.rem(me_c + k, n_cand)}, device_id_type=pl.DeviceIdType.MESH)

        copies[0].wait()
        copies[1].wait()
        for k in range(8):
            ccol[k * LANES:(k + 1) * LANES, :] = column_of(cover[k:k + 1, :] * 32.0)
            wcol[k * LANES:(k + 1) * LANES, :] = column_of(weights[k:k + 1, :] * (2.0 ** -20))
        copies[2].wait()
        column = (
            me_c * m
            + lax.broadcasted_iota(jnp.int32, (8, LANES), 0) * LANES
            + lax.broadcasted_iota(jnp.int32, (8, LANES), 1)
        )
        mask = jnp.full((8, LANES), -1e30, F32)
        for k in range(TOPK):
            mask = jnp.where(column == picks[k], 0.0, mask)
        bias[...] = mask
        copies[3].wait()
        copies[4].wait()

        sums = [jnp.zeros((8, LANES), F32) for _ in range(8)]

        def multiply(tile, rows, first):
            at = slice(rows * half, (rows + 1) * half)
            sims = lax.dot_general(
                points[at, :], cands[tile * 256:(tile + 1) * 256, :], (((1,), (1,)), ((), ())), preferred_element_type=F32
            )
            high = None
            for h in range(2):
                s = sims[:, h * LANES:(h + 1) * LANES]
                t = jnp.maximum(s - ccol[at, :], 0.0) * wcol[at, :]
                sums[2 * tile + h] = sums[2 * tile + h] + jnp.sum(t.reshape(half // 8, 8, LANES), axis=0)
                masked = s + bias[2 * tile + h:2 * tile + h + 1, :]
                high = masked if high is None else jnp.maximum(high, masked)
            maxes[at, :] = high if first else jnp.maximum(maxes[at, :], high)

        def send_parts(start, size):
            for k in range(start, start + size):
                part_out[k:k + 1, :] = jnp.sum(sums[k], axis=0, keepdims=True)
            part_in[me_p, start:start + size, :] = part_out[start:start + size, :]
            for peer in others:
                pltpu.make_async_remote_copy(
                    part_out.at[pl.ds(start, size)], part_in.at[me_p, pl.ds(start, size)], p_send, p_recv,
                    device_id={"pts": peer}, device_id_type=pl.DeviceIdType.MESH,
                ).start()

        multiply(0, 0, True)
        multiply(1, 0, False)
        copies[5].wait()
        copies[6].wait()
        multiply(0, 1, True)
        multiply(1, 1, False)
        for tile in (2, 3):
            for rows in (0, 1):
                multiply(tile, rows, False)
        pl.semaphore_wait(barrier, n_pts - 1 + len(beside))
        send_parts(0, 8)
        reach, rounds = near, 0
        while reach < n_cand // 2:
            for k in (reach, n_cand - reach):
                pl.semaphore_signal(
                    near_sem.at[rounds], 1, device_id={"cand": lax.rem(me_c + k, n_cand)}, device_id_type=pl.DeviceIdType.MESH
                )
            if rounds == 0:
                for k in range(8):
                    high = maxes[k * LANES:(k + 1) * LANES, :].T
                    cov_out[k:k + 1, :] = jnp.max(high, axis=0, keepdims=True) * (2.0 ** -5)
            pl.semaphore_wait(near_sem.at[rounds], 2)
            reach, rounds = 2 * reach, rounds + 1
        for k in along:
            pltpu.make_async_remote_copy(
                cov_out, cov_in.at[k], c_send, c_recv,
                device_id={"cand": lax.rem(me_c + k, n_cand)}, device_id_type=pl.DeviceIdType.MESH,
            ).start()

        some = part_in.at[pl.ds(0, n_pts - 1)]
        pltpu.make_async_copy(some, some, p_recv).wait()
        total = part_in[0]
        for k in range(1, n_pts):
            total = total + part_in[k]
        gains[...] = total
        top_out[...] = best_of_block(gains, col)
        for k in along:
            pltpu.make_async_remote_copy(
                top_out, top_in.at[k], t_send, t_recv.at[int(k == farthest)],
                device_id={"cand": lax.rem(me_c + k, n_cand)}, device_id_type=pl.DeviceIdType.MESH,
            ).start()

        some = cov_in.at[pl.ds(1, n_cand - 1)]
        pltpu.make_async_copy(some, some, c_recv).wait()
        best = jnp.maximum(cover[...], cov_out[...])
        for k in range(1, n_cand):
            best = jnp.maximum(best, cov_in[k])
        for k in range(8):
            gains_refs[k][...] = gains[k:k + 1, :]
            ncov_refs[k][...] = best[k:k + 1, :]

        some = top_in.at[pl.ds(0, n_cand - 2)]
        pltpu.make_async_copy(some, some, t_recv.at[0]).wait()
        top_near[...] = best_of_lists([top_out[...]] + [top_in[k] for k in range(1, n_cand) if k != farthest], col)

        for sent, sem, count in ((part_in, p_send, n_pts - 1), (cov_in, c_send, n_cand - 1), (top_in, t_send, n_cand - 1)):
            some = sent.at[pl.ds(0, count)]
            pltpu.make_async_copy(some, some, sem).wait()

    dma = pltpu.SemaphoreType.DMA
    pl.run_scoped(until_last_list, dma((7,)), dma, dma, dma)

    some = top_in.at[pl.ds(farthest, 1)]
    pltpu.make_async_copy(some, some, t_recv.at[1]).wait()
    top_ref[...] = best_of_lists([top_near[...], top_in[farthest]], col)


def write_out(*refs):
    rows, (gains, ncov, top), (gains_all, ncov_all, best, sem) = refs[:17], refs[17:20], refs[20:]
    best[...] = rows[16][:, :TOPK]
    for k in range(8):
        gains_all[k:k + 1, :] = rows[k][...]
        ncov_all[k:k + 1, :] = rows[8 + k][...]
    copies = [
        pltpu.make_async_copy(best, top, sem.at[0]),
        pltpu.make_async_copy(gains_all, gains, sem.at[1]),
        pltpu.make_async_copy(ncov_all, ncov, sem.at[2]),
    ]
    for copy in copies:
        copy.start()
    for copy in copies:
        copy.wait()


def on_device(points, weights, coverage, candidates, picks):
    n_pts, n_cand = lax.axis_size("pts"), lax.axis_size("cand")
    n, d = points.shape
    m = candidates.shape[0]
    hbm = pl.BlockSpec(memory_space=pl.ANY)
    vmem = pl.BlockSpec(memory_space=pltpu.VMEM)
    dma = pltpu.SemaphoreType.DMA
    inside = pl.pallas_call(
        functools.partial(kernel, n_pts, n_cand),
        out_shape=(jax.ShapeDtypeStruct((1, LANES), F32),) * 17,
        in_specs=[hbm] * 5,
        out_specs=(vmem,) * 17,
        scratch_shapes=[
            pltpu.VMEM((n, d), jnp.bfloat16),
            pltpu.VMEM((m, d), jnp.bfloat16),
            pltpu.VMEM((8, LANES), F32),
            pltpu.VMEM((8, LANES), F32),
            pltpu.SMEM((TOPK,), jnp.int32),
            pltpu.VMEM((n, LANES), F32),
            pltpu.VMEM((n, LANES), F32),
            pltpu.VMEM((8, LANES), F32),
            pltpu.VMEM((n, LANES), F32),
            pltpu.VMEM((1024, LANES), F32),
            pltpu.VMEM((8, LANES), F32),
            pltpu.VMEM((n_pts, 8, LANES), F32),
            pltpu.VMEM((8, LANES), F32),
            pltpu.VMEM((n_cand, 8, LANES), F32),
            pltpu.VMEM((1, LANES), F32),
            pltpu.VMEM((n_cand, 1, LANES), F32),
            pltpu.VMEM((1, LANES), F32),
            pltpu.VMEM((8, LANES), F32),
            dma, dma, dma((2,)), pltpu.SemaphoreType.REGULAR((1,)),
        ],
        compiler_params=pltpu.CompilerParams(
            collective_id=0, has_side_effects=True, vmem_limit_bytes=VMEM_BYTES
        ),
        name="facility",
    )(points, weights.reshape(8, LANES), coverage.reshape(8, LANES), candidates, picks)
    gains, ncov, top = pl.pallas_call(
        write_out,
        out_shape=(
            jax.ShapeDtypeStruct((8, LANES), F32),
            jax.ShapeDtypeStruct((8, LANES), F32),
            jax.ShapeDtypeStruct((1, TOPK), F32),
        ),
        in_specs=[vmem] * 17,
        out_specs=(hbm, hbm, hbm),
        scratch_shapes=[
            pltpu.VMEM((8, LANES), F32), pltpu.VMEM((8, LANES), F32), pltpu.VMEM((1, TOPK), F32), dma((3,))
        ],
        compiler_params=pltpu.CompilerParams(vmem_limit_bytes=2**20),
        name="write_out",
    )(*inside)
    return gains.reshape(m), top.reshape(TOPK), ncov.reshape(n)


def solution(mesh):
    placed = (P("pts", None), P("pts"), P("pts"), P("cand", None), P())
    return jax.shard_map(
        on_device, mesh=mesh, in_specs=placed, out_specs=(P("cand"), P(), P("pts")), check_vma=False
    )
```

time: 30.2 us -> 30.2 us (level)
  no operation moved by 1% of the time
where the time goes in v5:
time: 30.2 us; the launch traced here: 30 us
  Pallas kernels  29.4 us (97%)
  between operations  0.64 us (2%)
    pallas_call x1, Pallas kernels, on_device(): pl.pallas_call(functools.partial(kernel, n_pts, n_cand), out_shape=(jax.S...  28.8 us
    pallas_call x1, Pallas kernels, on_device(): pl.pallas_call(write_out, out_shape=(jax.ShapeDtypeStruct((8, LANES), F32...  0.64 us

profile of v5, /device:TPU:1, one launch (start us, length us, event | category | flops | bytes accessed | tf_op | source)
XLA Modules:
  0.0 30.0 jit_solution(3077898054843783621)
XLA Ops:
  0.6 28.8 %facility.1 = (f32[1,128]{1,0:T(1,128)S(1)}, f32[1,128]{1,0:T(1,128)S(1)}, f32[1,128]{1,0:T(1,128)S(1)}, f32[1,128]{1,0:T(1,128)S(1)}, f32[1,128]{1,0:T(1,128)S(...) custom-call(bf16[1024,1024]{1,0:T(8,128)(2,1)} %points_hbm.1, ...), custom_call_target="tpu_custom_call" | custom-call | tf_op jit(solution)/shard_map/facility/pallas_call | solution.py:288
  29.4 0.6 %write_out.1 = (f32[8,128]{1,0:T(8,128)}, f32[8,128]{1,0:T(8,128)}, f32[1,64]{1,0:T(1,128)}) custom-call(f32[1,128]{1,0:T(1,128)S(1)} %get-tuple-element.23.refs_0_, f32[1,128]{1,0:T(1,128)S(1)} %get-tuple-element.24.refs_1_, f32[1,128]{1,0:T(1,128)S(1)} %get-tuple-element.25.refs_2_, f32[1,128]{1,0:T(1,128)S(1)} %get-tuple-element.26.refs_3_, ...), custom_call_target="tpu_custom_call" | custom-call | tf_op jit(solution)/shard_map/write_out/pallas_call | solution.py:319

commit v6 on v5

--- a/solution.py
+++ b/solution.py
@@ -121,26 +121,28 @@
     ) = refs[17:]
     farthest = n_cand // 2
 
-    def until_last_list(in_sem, p_send, c_send, t_send):
-        n = points.shape[0]
+    def until_last_list(in_sem, p_send, c_send, t_send, *results):
+        n, d = points.shape
         m = cands.shape[0]
         me_p = lax.axis_index("pts")
         me_c = lax.axis_index("cand")
 
         half = n // 2
-        others = [k + lax.div(k - me_p + n_pts - 1, n_pts - 1) for k in range(n_pts - 1)]
         along = sorted(range(1, n_cand), key=lambda k: -min(k, n_cand - k))
         copies = [
             pltpu.make_async_copy(cover_hbm, cover, in_sem.at[0]),
             pltpu.make_async_copy(weights_hbm, weights, in_sem.at[1]),
             pltpu.make_async_copy(picks_hbm, picks, in_sem.at[2]),
             pltpu.make_async_copy(cand_hbm.at[pl.ds(0, m // 2)], cands.at[pl.ds(0, m // 2)], in_sem.at[3]),
-            pltpu.make_async_copy(points_hbm.at[pl.ds(0, half)], points.at[pl.ds(0, half)], in_sem.at[4]),
-            pltpu.make_async_copy(points_hbm.at[pl.ds(half, half)], points.at[pl.ds(half, half)], in_sem.at[5]),
-            pltpu.make_async_copy(cand_hbm.at[pl.ds(m // 2, m // 2)], cands.at[pl.ds(m // 2, m // 2)], in_sem.at[6]),
+            pltpu.make_async_copy(points_hbm.at[pl.ds(0, 256)], points.at[pl.ds(0, 256)], in_sem.at[4]),
+            pltpu.make_async_copy(points_hbm.at[pl.ds(256, 256)], points.at[pl.ds(256, 256)], in_sem.at[5]),
+            pltpu.make_async_copy(points_hbm.at[pl.ds(half, half)], points.at[pl.ds(half, half)], in_sem.at[6]),
+            pltpu.make_async_copy(cand_hbm.at[pl.ds(m // 2, m // 2)], cands.at[pl.ds(m // 2, m // 2)], in_sem.at[7]),
         ]
         for copy in copies:
             copy.start()
+
+        others = [k + lax.div(k - me_p + n_pts - 1, n_pts - 1) for k in range(n_pts - 1)]
 
         near = 4
         beside = [k for k in range(1, n_cand) if min(k, n_cand - k) <= near]
@@ -165,24 +167,49 @@
         for k in range(TOPK):
             mask = jnp.where(column == picks[k], 0.0, mask)
         bias[...] = mask
-        copies[3].wait()
-        copies[4].wait()
-
+        piece = 128
+        held = [[results[(2 * q + u) * 4:(2 * q + u) * 4 + 4] for q in range(2)] for u in range(2)]
+        for result in results:
+            pltpu.matmul_pop(result)
         sums = [jnp.zeros((8, LANES), F32) for _ in range(8)]
-
-        def multiply(tile, rows, first):
-            at = slice(rows * half, (rows + 1) * half)
-            sims = lax.dot_general(
-                points[at, :], cands[tile * 256:(tile + 1) * 256, :], (((1,), (1,)), ((), ())), preferred_element_type=F32
-            )
-            high = None
-            for h in range(2):
-                s = sims[:, h * LANES:(h + 1) * LANES]
-                t = jnp.maximum(s - ccol[at, :], 0.0) * wcol[at, :]
-                sums[2 * tile + h] = sums[2 * tile + h] + jnp.sum(t.reshape(half // 8, 8, LANES), axis=0)
-                masked = s + bias[2 * tile + h:2 * tile + h + 1, :]
-                high = masked if high is None else jnp.maximum(high, masked)
-            maxes[at, :] = high if first else jnp.maximum(maxes[at, :], high)
+        units = [(0, 256, 0, 4), (256, 256, 0, 5), (half, half, 0, 6), (0, half, 2, None), (half, half, 2, None)]
+        steps = [(unit, part) for unit in range(len(units)) for part in range(d // 256)]
+
+        def push(step):
+            unit, part = steps[step]
+            for q in range(2):
+                row = (units[unit][2] + q) * 256
+                pltpu.matmul_push_rhs(
+                    cands[row:row + 256, part * 256:(part + 1) * 256],
+                    staging_register=step % 2, mxu_index=q, transpose=True,
+                )
+
+        def accumulate(step):
+            unit, part = steps[step]
+            first, rows, _, _ = units[unit]
+            for p in range(rows // piece):
+                for q in range(2):
+                    pltpu.matmul_acc_lhs(
+                        held[unit % 2][q][p],
+                        points[first + p * piece:first + (p + 1) * piece, part * 256:(part + 1) * 256],
+                        load_staged_rhs=step % 2 if p == 0 else None,
+                    )
+
+        def finish(unit):
+            first, rows, tile, _ = units[unit]
+            for p in range(rows // piece):
+                at = slice(first + p * piece, first + (p + 1) * piece)
+                high = None
+                for q in range(2):
+                    sims = pltpu.matmul_pop(held[unit % 2][q][p])
+                    for h in range(2):
+                        lane = 2 * (tile + q) + h
+                        s = sims[:, h * LANES:(h + 1) * LANES]
+                        t = jnp.maximum(s - ccol[at, :], 0.0) * wcol[at, :]
+                        sums[lane] = sums[lane] + jnp.sum(t.reshape(piece // 8, 8, LANES), axis=0)
+                        masked = s + bias[lane:lane + 1, :]
+                        high = masked if high is None else jnp.maximum(high, masked)
+                maxes[at, :] = jnp.maximum(maxes[at, :], high) if tile else high
 
         def send_parts(start, size):
             for k in range(start, start + size):
@@ -194,15 +221,19 @@
                     device_id={"pts": peer}, device_id_type=pl.DeviceIdType.MESH,
                 ).start()
 
-        multiply(0, 0, True)
-        multiply(1, 0, False)
-        copies[5].wait()
-        copies[6].wait()
-        multiply(0, 1, True)
-        multiply(1, 1, False)
-        for tile in (2, 3):
-            for rows in (0, 1):
-                multiply(tile, rows, False)
+        copies[3].wait()
+        push(0)
+        for step, (unit, part) in enumerate(steps):
+            if step + 1 < len(steps):
+                if steps[step + 1] == (3, 0):
+                    copies[7].wait()
+                push(step + 1)
+            if part == 0 and units[unit][3] is not None:
+                copies[units[unit][3]].wait()
+            accumulate(step)
+            if part == 2 and unit > 0:
+                finish(unit - 1)
+        finish(len(units) - 1)
         pl.semaphore_wait(barrier, n_pts - 1 + len(beside))
         send_parts(0, 8)
         reach, rounds = near, 0
@@ -254,7 +285,8 @@
             pltpu.make_async_copy(some, some, sem).wait()
 
     dma = pltpu.SemaphoreType.DMA
-    pl.run_scoped(until_last_list, dma((7,)), dma, dma, dma)
+    products = [pltpu.ACC(q)((128, 256), F32) for q in range(2) for _ in range(8)]
+    pl.run_scoped(until_last_list, dma((8,)), dma, dma, dma, *products)
 
     some = top_in.at[pl.ds(farthest, 1)]
     pltpu.make_async_copy(some, some, t_recv.at[1]).wait()

time: 30.2 us -> 29.9 us (0.990)
  no operation moved by 1% of the time
where the time goes in v6:
time: 29.9 us; the launch traced here: 29.8 us
  Pallas kernels  29.2 us (98%)
  between operations  0.64 us (2%)
    pallas_call x1, Pallas kernels, on_device(): pl.pallas_call(functools.partial(kernel, n_pts, n_cand), out_shape=(jax.S...  28.5 us
    pallas_call x1, Pallas kernels, on_device(): pl.pallas_call(write_out, out_shape=(jax.ShapeDtypeStruct((8, LANES), F32...  0.64 us

profile of v6, /device:TPU:1, one launch (start us, length us, event | category | flops | bytes accessed | tf_op | source)
XLA Modules:
  0.0 29.8 jit_solution(1528382603509012317)
XLA Ops:
  0.6 28.5 %facility.1 = (f32[1,128]{1,0:T(1,128)S(1)}, f32[1,128]{1,0:T(1,128)S(1)}, f32[1,128]{1,0:T(1,128)S(1)}, f32[1,128]{1,0:T(1,128)S(1)}, f32[1,128]{1,0:T(1,128)S(...) custom-call(bf16[1024,1024]{1,0:T(8,128)(2,1)} %points_hbm.1, ...), custom_call_target="tpu_custom_call" | custom-call | tf_op jit(solution)/shard_map/facility/pallas_call | solution.py:320
  29.2 0.6 %write_out.1 = (f32[8,128]{1,0:T(8,128)}, f32[8,128]{1,0:T(8,128)}, f32[1,64]{1,0:T(1,128)}) custom-call(f32[1,128]{1,0:T(1,128)S(1)} %get-tuple-element.23.refs_0_, f32[1,128]{1,0:T(1,128)S(1)} %get-tuple-element.24.refs_1_, f32[1,128]{1,0:T(1,128)S(1)} %get-tuple-element.25.refs_2_, f32[1,128]{1,0:T(1,128)S(1)} %get-tuple-element.26.refs_3_, ...), custom_call_target="tpu_custom_call" | custom-call | tf_op jit(solution)/shard_map/write_out/pallas_call | solution.py:351

commit v7 on v6

--- a/solution.py
+++ b/solution.py
@@ -78,13 +78,27 @@
 def best_of_block(total_ref, col_ref):
     sub, lane, _ = positions()
     rows = descending([total_ref[k:k + 1, :] for k in range(8)])
-    for k, row in enumerate(rows):
-        col_ref[k * LANES:(k + 1) * LANES, :] = column_of(row)
+    ranked = ((0, (0,)), (1, (1, 2)), (3, (3, 4, 5, 6, 7)))
+    for k, _ in ranked:
+        col_ref[k * LANES:(k + 1) * LANES, :] = column_of(rows[k])
     kept = []
-    for k, row in enumerate(rows):
+    for k, taken in ranked:
+        row = wide(rows[k])
         columns = [col_ref[k * LANES + 8 * j:k * LANES + 8 * j + 8, :] for j in range(16)]
-        above = number_above(columns, wide(row))
-        kept += placed([(wide(row), above)], -(-(TOPK // (k + 1)) // 8), sub)
+        blocks = TOPK // (k + 1) // 8
+        if taken == (k,):
+            kept += placed([(row, number_above(columns, row))], blocks, sub)
+            continue
+        before = [
+            jnp.where((column > row) | ((column == row) & (sub + float(8 * j) < lane)), 1.0, 0.0)
+            for j, column in enumerate(columns)
+        ]
+        rank = wide(jnp.sum(added(before), axis=0, keepdims=True))
+        for block in range(blocks):
+            here = rank == sub + float(8 * block)
+            for r in taken:
+                best = jnp.max(jnp.where(here, wide(rows[r]), -jnp.inf), axis=1, keepdims=True)
+                kept.append(jnp.broadcast_to(best, (8, LANES)))
     first = as_row(kept[:16], sub, lane)
     second = jnp.where(lane[:1] < 8.0 * (len(kept) - 16), as_row(kept[16:], sub, lane), -jnp.inf)
     return order_pair([first, second], kept)
@@ -256,9 +270,7 @@
 
         some = part_in.at[pl.ds(0, n_pts - 1)]
         pltpu.make_async_copy(some, some, p_recv).wait()
-        total = part_in[0]
-        for k in range(1, n_pts):
-            total = total + part_in[k]
+        total = added([part_in[k] for k in range(n_pts)])
         gains[...] = total
         top_out[...] = best_of_block(gains, col)
         for k in along:
@@ -294,20 +306,24 @@
 
 
 def write_out(*refs):
-    rows, (gains, ncov, top), (gains_all, ncov_all, best, sem) = refs[:17], refs[17:20], refs[20:]
+    rows, (gains, ncov, top), (gains_all, ncov_all, best) = refs[:17], refs[17:20], refs[20:]
     best[...] = rows[16][:, :TOPK]
     for k in range(8):
         gains_all[k:k + 1, :] = rows[k][...]
         ncov_all[k:k + 1, :] = rows[8 + k][...]
-    copies = [
-        pltpu.make_async_copy(best, top, sem.at[0]),
-        pltpu.make_async_copy(gains_all, gains, sem.at[1]),
-        pltpu.make_async_copy(ncov_all, ncov, sem.at[2]),
-    ]
-    for copy in copies:
-        copy.start()
-    for copy in copies:
-        copy.wait()
+
+    def send(sem):
+        copies = [
+            pltpu.make_async_copy(best, top, sem.at[0]),
+            pltpu.make_async_copy(gains_all, gains, sem.at[1]),
+            pltpu.make_async_copy(ncov_all, ncov, sem.at[2]),
+        ]
+        for copy in copies:
+            copy.start()
+        for copy in copies:
+            copy.wait()
+
+    pl.run_scoped(send, pltpu.SemaphoreType.DMA((3,)))
 
 
 def on_device(points, weights, coverage, candidates, picks):
@@ -358,7 +374,7 @@
         in_specs=[vmem] * 17,
         out_specs=(hbm, hbm, hbm),
         scratch_shapes=[
-            pltpu.VMEM((8, LANES), F32), pltpu.VMEM((8, LANES), F32), pltpu.VMEM((1, TOPK), F32), dma((3,))
+            pltpu.VMEM((8, LANES), F32), pltpu.VMEM((8, LANES), F32), pltpu.VMEM((1, TOPK), F32)
         ],
         compiler_params=pltpu.CompilerParams(vmem_limit_bytes=2**20),
         name="write_out",

time: 29.9 us -> 29.8 us (level)
  no operation moved by 1% of the time
where the time goes in v7:
time: 29.8 us; the launch traced here: 29.7 us
  Pallas kernels  29.1 us (98%)
  between operations  0.64 us (2%)
    pallas_call x1, Pallas kernels, on_device(): pl.pallas_call(functools.partial(kernel, n_pts, n_cand), out_shape=(jax.S...  28.4 us
    pallas_call x1, Pallas kernels, on_device(): pl.pallas_call(write_out, out_shape=(jax.ShapeDtypeStruct((8, LANES), F32...  0.62 us

profile of v7, /device:TPU:1, one launch (start us, length us, event | category | flops | bytes accessed | tf_op | source)
XLA Modules:
  0.0 29.7 jit_solution(11640947760564533339)
XLA Ops:
  0.6 28.4 %facility.1 = (f32[1,128]{1,0:T(1,128)S(1)}, f32[1,128]{1,0:T(1,128)S(1)}, f32[1,128]{1,0:T(1,128)S(1)}, f32[1,128]{1,0:T(1,128)S(1)}, f32[1,128]{1,0:T(1,128)S(...) custom-call(bf16[1024,1024]{1,0:T(8,128)(2,1)} %points_hbm.1, ...), custom_call_target="tpu_custom_call" | custom-call | tf_op jit(solution)/shard_map/facility/pallas_call | solution.py:336
  29.1 0.6 %write_out.1 = (f32[8,128]{1,0:T(8,128)}, f32[8,128]{1,0:T(8,128)}, f32[1,64]{1,0:T(1,128)}) custom-call(f32[1,128]{1,0:T(1,128)S(1)} %get-tuple-element.23.refs_0_, f32[1,128]{1,0:T(1,128)S(1)} %get-tuple-element.24.refs_1_, f32[1,128]{1,0:T(1,128)S(1)} %get-tuple-element.25.refs_2_, f32[1,128]{1,0:T(1,128)S(1)} %get-tuple-element.26.refs_3_, ...), custom_call_target="tpu_custom_call" | custom-call | tf_op jit(solution)/shard_map/write_out/pallas_call | solution.py:367

commit v8 on v7

--- a/solution.py
+++ b/solution.py
@@ -126,11 +126,27 @@
     return order_pair([line for line, _ in packed], columns)
 
 
+def merge_last(far, near_columns):
+    sub, lane, twice = positions()
+    row, first = wide(far), lane < float(TOPK)
+    parts, ahead = [], []
+    for block, column in enumerate(near_columns):
+        count = jnp.sum(jnp.where((row > column) & first, 1.0, 0.0), axis=1, keepdims=True)
+        parts.append(jnp.where(count + sub + float(8 * block) == lane, column, 0.0))
+        ahead.append(jnp.where(column >= row, 1.0, 0.0))
+    place = wide(jnp.sum(added(ahead), axis=0, keepdims=True)) + twice
+    for block in range(TOPK // 8):
+        slot = sub + float(8 * block)
+        value = jnp.sum(jnp.where((place == slot) & first, row, 0.0), axis=1, keepdims=True)
+        parts.append(jnp.where(lane == slot, value, 0.0))
+    return jnp.sum(added(parts), axis=0, keepdims=True)
+
+
 def kernel(n_pts, n_cand, points_hbm, weights_hbm, cover_hbm, cand_hbm, picks_hbm, *refs):
     gains_refs, ncov_refs, top_ref = refs[:8], refs[8:16], refs[16]
     (
         points, cands, weights, cover, picks, wcol, ccol, bias, maxes, col,
-        part_out, part_in, cov_out, cov_in, top_out, top_in, top_near, gains,
+        part_out, part_in, cov_out, cov_in, top_out, top_in, near_columns, gains,
         p_recv, c_recv, t_recv, near_sem,
     ) = refs[17:]
     farthest = n_cand // 2
@@ -290,7 +306,8 @@
 
         some = top_in.at[pl.ds(0, n_cand - 2)]
         pltpu.make_async_copy(some, some, t_recv.at[0]).wait()
-        top_near[...] = best_of_lists([top_out[...]] + [top_in[k] for k in range(1, n_cand) if k != farthest], col)
+        near = best_of_lists([top_out[...]] + [top_in[k] for k in range(1, n_cand) if k != farthest], col)
+        near_columns[...] = column_of(near)[:TOPK, :]
 
         for sent, sem, count in ((part_in, p_send, n_pts - 1), (cov_in, c_send, n_cand - 1), (top_in, t_send, n_cand - 1)):
             some = sent.at[pl.ds(0, count)]
@@ -302,7 +319,7 @@
 
     some = top_in.at[pl.ds(farthest, 1)]
     pltpu.make_async_copy(some, some, t_recv.at[1]).wait()
-    top_ref[...] = best_of_lists([top_near[...], top_in[farthest]], col)
+    top_ref[...] = merge_last(top_in[farthest], [near_columns[k:k + 8, :] for k in range(0, TOPK, 8)])
 
 
 def write_out(*refs):
@@ -355,7 +372,7 @@
             pltpu.VMEM((n_cand, 8, LANES), F32),
             pltpu.VMEM((1, LANES), F32),
             pltpu.VMEM((n_cand, 1, LANES), F32),
-            pltpu.VMEM((1, LANES), F32),
+            pltpu.VMEM((TOPK, LANES), F32),
             pltpu.VMEM((8, LANES), F32),
             dma, dma, dma((2,)), pltpu.SemaphoreType.REGULAR((1,)),
         ],

time: 29.8 us -> 29.8 us (level)
  no operation moved by 1% of the time
where the time goes in v8:
time: 29.8 us; the launch traced here: 29.7 us
  Pallas kernels  29 us (97%)
  between operations  0.64 us (2%)
    pallas_call x1, Pallas kernels, on_device(): pl.pallas_call(functools.partial(kernel, n_pts, n_cand), out_shape=(jax.S...  28.4 us
    pallas_call x1, Pallas kernels, on_device(): pl.pallas_call(write_out, out_shape=(jax.ShapeDtypeStruct((8, LANES), F32...  0.62 us

profile of v8, /device:TPU:1, one launch (start us, length us, event | category | flops | bytes accessed | tf_op | source)
XLA Modules:
  0.0 29.7 jit_solution(10398440966549407921)
XLA Ops:
  0.6 28.4 %facility.1 = (f32[1,128]{1,0:T(1,128)S(1)}, f32[1,128]{1,0:T(1,128)S(1)}, f32[1,128]{1,0:T(1,128)S(1)}, f32[1,128]{1,0:T(1,128)S(1)}, f32[1,128]{1,0:T(1,128)S(...) custom-call(bf16[1024,1024]{1,0:T(8,128)(2,1)} %points_hbm.1, ...), custom_call_target="tpu_custom_call" | custom-call | tf_op jit(solution)/shard_map/facility/pallas_call | solution.py:353
  29.0 0.6 %write_out.1 = (f32[8,128]{1,0:T(8,128)}, f32[8,128]{1,0:T(8,128)}, f32[1,64]{1,0:T(1,128)}) custom-call(f32[1,128]{1,0:T(1,128)S(1)} %get-tuple-element.23.refs_0_, f32[1,128]{1,0:T(1,128)S(1)} %get-tuple-element.24.refs_1_, f32[1,128]{1,0:T(1,128)S(1)} %get-tuple-element.25.refs_2_, f32[1,128]{1,0:T(1,128)S(1)} %get-tuple-element.26.refs_3_, ...), custom_call_target="tpu_custom_call" | custom-call | tf_op jit(solution)/shard_map/write_out/pallas_call | solution.py:384

commit v9 on v8

--- a/solution.py
+++ b/solution.py
@@ -244,12 +244,12 @@
         def send_parts(start, size):
             for k in range(start, start + size):
                 part_out[k:k + 1, :] = jnp.sum(sums[k], axis=0, keepdims=True)
-            part_in[me_p, start:start + size, :] = part_out[start:start + size, :]
             for peer in others:
                 pltpu.make_async_remote_copy(
                     part_out.at[pl.ds(start, size)], part_in.at[me_p, pl.ds(start, size)], p_send, p_recv,
                     device_id={"pts": peer}, device_id_type=pl.DeviceIdType.MESH,
                 ).start()
+            part_in[me_p, start:start + size, :] = part_out[start:start + size, :]
 
         copies[3].wait()
         push(0)

time: 29.8 us -> 29.8 us (level)
  no operation moved by 1% of the time
where the time goes in v9:
time: 29.8 us; the launch traced here: 29.7 us
  Pallas kernels  29 us (97%)
  between operations  0.64 us (2%)
    pallas_call x1, Pallas kernels, on_device(): pl.pallas_call(functools.partial(kernel, n_pts, n_cand), out_shape=(jax.S...  28.4 us
    pallas_call x1, Pallas kernels, on_device(): pl.pallas_call(write_out, out_shape=(jax.ShapeDtypeStruct((8, LANES), F32...  0.62 us

profile of v9, /device:TPU:1, one launch (start us, length us, event | category | flops | bytes accessed | tf_op | source)
XLA Modules:
  0.0 29.7 jit_solution(17745777974080698996)
XLA Ops:
  0.6 28.4 %facility.1 = (f32[1,128]{1,0:T(1,128)S(1)}, f32[1,128]{1,0:T(1,128)S(1)}, f32[1,128]{1,0:T(1,128)S(1)}, f32[1,128]{1,0:T(1,128)S(1)}, f32[1,128]{1,0:T(1,128)S(...) custom-call(bf16[1024,1024]{1,0:T(8,128)(2,1)} %points_hbm.1, ...), custom_call_target="tpu_custom_call" | custom-call | tf_op jit(solution)/shard_map/facility/pallas_call | solution.py:353
  29.0 0.6 %write_out.1 = (f32[8,128]{1,0:T(8,128)}, f32[8,128]{1,0:T(8,128)}, f32[1,64]{1,0:T(1,128)}) custom-call(f32[1,128]{1,0:T(1,128)S(1)} %get-tuple-element.23.refs_0_, f32[1,128]{1,0:T(1,128)S(1)} %get-tuple-element.24.refs_1_, f32[1,128]{1,0:T(1,128)S(1)} %get-tuple-element.25.refs_2_, f32[1,128]{1,0:T(1,128)S(1)} %get-tuple-element.26.refs_3_, ...), custom_call_target="tpu_custom_call" | custom-call | tf_op jit(solution)/shard_map/write_out/pallas_call | solution.py:384
